TPU v7x, 32 devices: a whole 2x2x4 slice. The times are simulated.
32 devices in a mesh: sims: 2 (over x), rows: 4 (over y, core), fields: 4 (over z).
Axes of the slice: x: 2, y: 2, z: 4, core: 2. Of those that a mesh axis runs over, the one named last changes fastest.
Arguments:
- sky_maps: float32 [6, 32, 16384], P('sims', 'rows', 'fields'), parts along dimension 0, may hold values from -7 to 7
- band_cuts: int32 [6], replicated, may hold values from 1 to 8191, as said below
- filters: float32 [3, 32, 16384], P(None, ('rows', 'fields')), may hold values from 0.3 to 3
- wiener: float32 [2, 32, 16384], P(None, ('rows', 'fields')), may hold values from 0.3 to 3
- response: float32 [32, 16384], P(('rows', 'fields')), may hold values from 0.5 to 2
Outputs:
- phi_curl: float32 [4, 32, 16384], P('sims', 'rows', 'fields'), parts along dimension 0
There are 2 independent parts, one for each index of `sims`. A program takes and returns all parts, laid end to end along the dimension named above; an argument that names none is the same for every part. Nothing has to cross between parts.
Inputs may be any that keep to these rules, and one draw needn't show every extreme that they name: `band_cuts`: entries 0, 2 and 4 are the smallest multipole indices of the temperature, polarization and estimate bands and lie below 512; entries 1, 3 and 5 are the largest and are at least 4096.
All inputs are finite; a program needn't handle non-finite values.
Results may differ from a plain program's by a relative error of at most 0.00019.
Values sent between devices are 32-bit elements; how exact they have to be, the bound alone decides.
A program may use at most 128 MiB of HBM per device.

v0:
```python
import functools
import math

import jax
import jax.numpy as jnp
import numpy as np
from jax import lax
from jax.experimental import pallas as pl
from jax.experimental.pallas import tpu as pltpu
from jax.sharding import PartitionSpec as P

NC = 16384


exact_mode = lax.Precision.HIGHEST


def split_factor(length):
    best_first = 1
    for divisor in range(1, math.isqrt(length) + 1):
        if length % divisor == 0:
            best_first = divisor
    return (best_first, length // best_first)


def phase_table(left_index, right_index, period, direction):
    product = left_index[:, None] * right_index[None, :] % period
    angles = direction * 2.0 * math.pi / period * product.astype(jnp.float32)
    return (jnp.cos(angles), jnp.sin(angles))


def complex_einsum(formula, data_pair, table_pair):
    data_real, data_imag = data_pair
    table_real, table_imag = table_pair
    real_out = jnp.einsum(formula, data_real, table_real, precision=exact_mode)
    imag_out = jnp.einsum(formula, data_real, table_imag, precision=exact_mode)
    if data_imag is not None:
        real_out = real_out - jnp.einsum(formula, data_imag, table_imag, precision=exact_mode)
        imag_out = imag_out + jnp.einsum(formula, data_imag, table_real, precision=exact_mode)
    return (real_out, imag_out)


def complex_mul(left_pair, right_pair):
    return (
        left_pair[0] * right_pair[0] - left_pair[1] * right_pair[1],
        left_pair[0] * right_pair[1] + left_pair[1] * right_pair[0],
    )


def conj_mul(left_pair, right_pair):
    return (
        left_pair[0] * right_pair[0] + left_pair[1] * right_pair[1],
        left_pair[0] * right_pair[1] - left_pair[1] * right_pair[0],
    )


def row_transform(data_pair, direction):
    batch_len, length, block_width = data_pair[0].shape
    outer_len, inner_len = split_factor(length)
    outer_ids = jnp.arange(outer_len, dtype=jnp.int32)
    inner_ids = jnp.arange(inner_len, dtype=jnp.int32)
    real_in = data_pair[0].reshape(batch_len, outer_len, inner_len, block_width)
    imag_in = None
    if data_pair[1] is not None:
        imag_in = data_pair[1].reshape(batch_len, outer_len, inner_len, block_width)
    middle = complex_einsum(
        "bjmc,jk->bkmc", (real_in, imag_in), phase_table(outer_ids, outer_ids, outer_len, direction)
    )
    twiddle = phase_table(outer_ids, inner_ids, length, direction)
    middle = complex_mul(middle, (twiddle[0][None, :, :, None], twiddle[1][None, :, :, None]))
    result = complex_einsum(
        "bkmc,mq->bqkc", middle, phase_table(inner_ids, inner_ids, inner_len, direction)
    )
    norm_factor = 1.0 if direction < 0 else 1.0 / length
    return (
        result[0].reshape(batch_len, length, block_width) * norm_factor,
        result[1].reshape(batch_len, length, block_width) * norm_factor,
    )


def block_order(groups, fields_count):
    positions = jnp.arange(groups, dtype=jnp.int32)
    blocks = positions % fields_count * (groups // fields_count) + positions // fields_count
    return (positions, blocks)


def column_forward(data_pair, groups, fields_count):
    batch_len, local_rows, total_len = data_pair[0].shape
    block_width = total_len // groups
    positions, blocks = block_order(groups, fields_count)
    column_ids = jnp.arange(block_width, dtype=jnp.int32)
    shaped = (
        data_pair[0].reshape(batch_len, local_rows, groups, block_width),
        data_pair[1].reshape(batch_len, local_rows, groups, block_width),
    )
    middle = complex_einsum("brpc,pk->brkc", shaped, phase_table(blocks, positions, groups, -1.0))
    twiddle = phase_table(positions, column_ids, total_len, -1.0)
    middle = complex_mul(middle, (twiddle[0][None, None], twiddle[1][None, None]))
    result = complex_einsum(
        "brkc,cq->brqk", middle, phase_table(column_ids, column_ids, block_width, -1.0)
    )
    return (
        result[0].reshape(batch_len, local_rows, total_len),
        result[1].reshape(batch_len, local_rows, total_len),
    )


def column_inverse(data_pair, groups, fields_count):
    batch_len, local_rows, total_len = data_pair[0].shape
    block_width = total_len // groups
    positions, blocks = block_order(groups, fields_count)
    column_ids = jnp.arange(block_width, dtype=jnp.int32)
    shaped = (
        data_pair[0].reshape(batch_len, local_rows, block_width, groups),
        data_pair[1].reshape(batch_len, local_rows, block_width, groups),
    )
    middle = complex_einsum(
        "brqk,qc->brkc", shaped, phase_table(column_ids, column_ids, block_width, 1.0)
    )
    twiddle = phase_table(positions, column_ids, total_len, 1.0)
    middle = complex_mul(middle, (twiddle[0][None, None], twiddle[1][None, None]))
    result = complex_einsum("brkc,kp->brpc", middle, phase_table(positions, blocks, groups, 1.0))
    norm_factor = 1.0 / total_len
    return (
        result[0].reshape(batch_len, local_rows, total_len) * norm_factor,
        result[1].reshape(batch_len, local_rows, total_len) * norm_factor,
    )


def body(sky_maps, band_cuts, filters, wiener, response):
    rows_count = lax.axis_size("rows")
    fields_count = lax.axis_size("fields")
    groups = rows_count * fields_count
    local_rows = filters.shape[1]
    total_rows = local_rows * groups
    row_ratio = NC // total_rows

    def forward_columns(stacked):
        return jnp.stack(column_forward((stacked[0], stacked[1]), groups, fields_count))

    def inverse_rows(stacked):
        return jnp.stack(row_transform((stacked[0], stacked[1]), 1.0))

    def inverse_columns(stacked):
        return jnp.stack(column_inverse((stacked[0], stacked[1]), groups, fields_count))

    def to_frequency(stacked):
        batch_len = stacked.shape[1]
        block_width = stacked.shape[3]
        shaped = stacked.reshape(
            2, batch_len, rows_count, fields_count, local_rows, 1, 1, block_width
        )
        arrived = lax.all_to_all(
            lax.all_to_all(shaped, "rows", split_axis=2, concat_axis=5, tiled=True),
            "fields",
            split_axis=3,
            concat_axis=6,
            tiled=True,
        )
        result = forward_columns(arrived.reshape(2, batch_len, local_rows, groups * block_width))
        return result

    def to_space(stacked):
        batch_len = stacked.shape[1]
        block_width = stacked.shape[3] // groups
        shaped = stacked.reshape(
            2, batch_len, 1, 1, local_rows, rows_count, fields_count, block_width
        )
        arrived = lax.all_to_all(
            lax.all_to_all(shaped, "rows", split_axis=5, concat_axis=2, tiled=True),
            "fields",
            split_axis=6,
            concat_axis=3,
            tiled=True,
        )
        result = inverse_rows(arrived.reshape(2, batch_len, total_rows, block_width))
        return result

    slab_spectra = jnp.stack(
        row_transform(
            (lax.all_to_all(sky_maps, "rows", split_axis=2, concat_axis=1, tiled=True), None), -1.0
        )
    )
    sky_spectra = to_frequency(slab_spectra)
    row_ids = lax.axis_index(("rows", "fields")) * local_rows + jnp.arange(
        local_rows, dtype=jnp.int32
    )
    freq_rows = jnp.where(row_ids < total_rows // 2, row_ids, row_ids - total_rows)[:, None]
    column_ids = jnp.arange(NC, dtype=jnp.int32)
    freq_cols = jnp.where(column_ids < NC // 2, column_ids, column_ids - NC)[None, :]
    scaled_rows = row_ratio * freq_rows
    radius_sq = freq_cols * freq_cols + scaled_rows * scaled_rows

    def band_mask(lower_cut, upper_cut):
        inside = (radius_sq >= lower_cut * lower_cut) & (radius_sq <= upper_cut * upper_cut)
        return inside.astype(jnp.float32)

    mask_temp = band_mask(band_cuts[0], band_cuts[1])
    mask_pol = band_mask(band_cuts[2], band_cuts[3])
    mask_out = band_mask(band_cuts[4], band_cuts[5])
    radius_floor = jnp.maximum(radius_sq, 1).astype(jnp.float32)
    cos_two = (freq_cols * freq_cols - scaled_rows * scaled_rows).astype(jnp.float32) / radius_floor
    sin_two = (2 * freq_cols * scaled_rows).astype(jnp.float32) / radius_floor
    along_x = (2 * freq_cols).astype(jnp.float32) / NC
    along_y = (2 * freq_rows).astype(jnp.float32) / total_rows
    raising = (-along_y + 0.0 * along_x, along_x + 0.0 * along_y)
    lowering = (along_y + 0.0 * along_x, along_x + 0.0 * along_y)
    rotation = (cos_two, sin_two)
    temp_modes = (sky_spectra[0, 0], sky_spectra[1, 0])
    stokes_q = (sky_spectra[0, 1], sky_spectra[1, 1])
    stokes_u = (sky_spectra[0, 2], sky_spectra[1, 2])
    e_modes = (
        -(cos_two * stokes_q[0] + sin_two * stokes_u[0]),
        -(cos_two * stokes_q[1] + sin_two * stokes_u[1]),
    )
    b_modes = (
        sin_two * stokes_q[0] - cos_two * stokes_u[0],
        sin_two * stokes_q[1] - cos_two * stokes_u[1],
    )
    temp_weight = mask_temp * filters[0]
    e_weight = mask_pol * filters[1]
    b_weight = mask_pol * filters[2]
    temp_bar = (temp_weight * temp_modes[0], temp_weight * temp_modes[1])
    e_bar = (e_weight * e_modes[0], e_weight * e_modes[1])
    b_bar = (b_weight * b_modes[0], b_weight * b_modes[1])
    grad_temp = complex_mul(raising, (wiener[0] * temp_bar[0], wiener[0] * temp_bar[1]))
    pol_sum = complex_mul((e_bar[0] - b_bar[1], e_bar[1] + b_bar[0]), rotation)
    pol_bar = (-pol_sum[0], -pol_sum[1])
    pol_rot = complex_mul((wiener[1] * e_bar[0], wiener[1] * e_bar[1]), rotation)
    pol_wiener = (-pol_rot[0], -pol_rot[1])
    spin_three = complex_mul(raising, pol_wiener)
    spin_one = complex_mul(lowering, pol_wiener)
    leg_spectra = jnp.stack(
        [
            jnp.stack([temp_bar[0], grad_temp[0], pol_bar[0], spin_three[0], spin_one[0]]),
            jnp.stack([temp_bar[1], grad_temp[1], pol_bar[1], spin_three[1], spin_one[1]]),
        ]
    )
    leg_maps = to_space(inverse_columns(leg_spectra))
    temp_leg = (leg_maps[0, 0], leg_maps[1, 0])
    grad_leg = (leg_maps[0, 1], leg_maps[1, 1])
    pol_leg = (leg_maps[0, 2], leg_maps[1, 2])
    three_leg = (leg_maps[0, 3], leg_maps[1, 3])
    one_leg = (leg_maps[0, 4], leg_maps[1, 4])
    temp_term = complex_mul(temp_leg, grad_leg)
    raise_term = conj_mul(pol_leg, three_leg)
    lower_term = conj_mul(one_leg, pol_leg)
    current = (
        temp_term[0] + 0.5 * (raise_term[0] + lower_term[0]),
        temp_term[1] + 0.5 * (raise_term[1] + lower_term[1]),
    )
    current_rows = jnp.stack(row_transform((current[0][None], current[1][None]), -1.0))
    current_modes = to_frequency(current_rows)
    out_weight = mask_out * response
    estimate_modes = complex_mul(
        lowering, (out_weight * current_modes[0, 0], out_weight * current_modes[1, 0])
    )
    estimate_stack = jnp.stack([estimate_modes[0][None], estimate_modes[1][None]])
    estimate_maps = to_space(inverse_columns(estimate_stack))
    slab_result = estimate_maps[:, 0]
    return lax.all_to_all(slab_result, "rows", split_axis=1, concat_axis=2, tiled=True)


SIDE = 128
TILE = (8, 128)
LEG_GROUPS = ((0, 2), (2, 2), (4, 1))
MESH = pl.DeviceIdType.MESH


def add_pair(a, b):
    imag = a[1] if b[1] is None else b[1] if a[1] is None else a[1] + b[1]
    return (a[0] + b[0], imag)


def sub_pair(a, b):
    imag = a[1] if b[1] is None else -b[1] if a[1] is None else a[1] - b[1]
    return (a[0] - b[0], imag)


def turn_pair(value, step, length, direction):
    real, imag = value
    if step == 0:
        return value
    if 4 * step == length:
        if imag is None:
            return (jnp.zeros_like(real), real if direction > 0 else -real)
        return (-imag, real) if direction > 0 else (imag, -real)
    angle = 2.0 * math.pi * step / length
    c, s = math.cos(angle), direction * math.sin(angle)
    if imag is None:
        return (real * c, real * s)
    if 8 * step == length:
        if direction > 0:
            return ((real - imag) * c, (real + imag) * c)
        return ((real + imag) * c, (imag - real) * c)
    if 8 * step == 3 * length:
        if direction > 0:
            return ((real + imag) * c, (imag - real) * c)
        return ((real - imag) * c, (real + imag) * c)
    return (real * c - imag * s, real * s + imag * c)


def short_transform(values, direction):
    length = len(values)
    if length == 1:
        return values
    even = short_transform(values[0::2], direction)
    odd = short_transform(values[1::2], direction)
    low, high = [], []
    for step in range(length // 2):
        turned = turn_pair(odd[step], step, length, direction)
        low.append(add_pair(even[step], turned))
        high.append(sub_pair(even[step], turned))
    return low + high


def split_number(x):
    top = x.astype(jnp.bfloat16)
    return top, (x - top.astype(jnp.float32)).astype(jnp.bfloat16)


def dot32(a, b):
    return jnp.dot(a, b, preferred_element_type=jnp.float32)


def matrix_left(table_ref, which, x):
    top, rest = split_number(x)
    m_top, m_rest = table_ref[which, 0], table_ref[which, 1]
    return dot32(m_top, top) + (dot32(m_top, rest) + dot32(m_rest, top))


def matrix_right(table_ref, which, x):
    top, rest = split_number(x)
    m_top, m_rest = table_ref[which, 0], table_ref[which, 1]
    return dot32(top, m_top) + (dot32(top, m_rest) + dot32(rest, m_top))


def lens_kernel(
    rows_count, fields_count, local_rows,
    cuts_ref, sky_hbm, filters_hbm, wiener_hbm, response_hbm, table_ref, twiddle_ref, out_ref,
    sky_ref, raw, weight_ref, slab_out, slab_in, spec_out, spec_in, weights, legs_out, legs_in, maps, current,
    cur_out, cur_in, est_out, est_in, fin_out, fin_in,
    slab_sem, spec_sem, legs_sem, cur_sem, est_sem, fin_sem, self_sem, load_sem,
):
    groups = rows_count * fields_count
    total_rows = groups * local_rows
    in_rows = total_rows // rows_count
    row_ratio = NC // total_rows
    my_r, my_f = lax.axis_index("rows"), lax.axis_index("fields")
    me = my_r * fields_count + my_f
    my_block = my_f * rows_count + my_r

    half = fields_count // 2
    my_half, my_spot = my_f // half, my_f % half

    def wrapped(value, length):
        return jnp.where(value >= length, value - length, value)

    row_at = [wrapped(my_r + d, rows_count) for d in range(rows_count)]
    spot_at = [wrapped(my_spot + d, half) for d in range(half)]
    side_at = [my_half * half, (1 - my_half) * half]

    def partner(q, sign):
        side = 1 - q // (rows_count * half)
        spot = sign * (q // rows_count + 1) % half
        return row_at[sign * (q + 1) % rows_count], side_at[side] + spot_at[spot]

    def peer_of(q):
        r, f = partner(q, 1)
        return r * fields_count + f

    def source_of(q):
        r, f = partner(q, -1)
        return r * fields_count + f

    def peer_block(q):
        r, f = partner(q, 1)
        return f * rows_count + r

    def source_block(q):
        r, f = partner(q, -1)
        return f * rows_count + r

    def target(q):
        r, f = partner(q, 1)
        return {"rows": r, "fields": f}

    def send(q, src, dst, sems):
        return pltpu.make_async_remote_copy(
            src_ref=src, dst_ref=dst, send_sem=sems[0], recv_sem=sems[1],
            device_id=target(q), device_id_type=MESH,
        )

    def send_row(q, src, dst, sems):
        return pltpu.make_async_remote_copy(
            src_ref=src, dst_ref=dst, send_sem=sems[0], recv_sem=sems[1],
            device_id={"rows": row_at[q]}, device_id_type=MESH,
        )

    def each_peer(body):
        for q in range(groups - 1):
            body(q)

    def each_row_peer(body):
        for q in range(1, rows_count):
            body(q)

    loads = [
        pltpu.make_async_copy(src, dst, load_sem.at[n])
        for n, (src, dst) in enumerate((
            (sky_hbm, sky_ref),
            (filters_hbm, raw.at[0:3]),
            (wiener_hbm, raw.at[3:5]),
            (response_hbm, raw.at[5]),
        ))
    ]
    for load in loads:
        load.start()

    barrier = pltpu.get_barrier_semaphore()

    def greet(q):
        pl.semaphore_signal(
            barrier, inc=1, device_id=target(q), device_id_type=MESH
        )

    each_peer(greet)
    loads[0].wait()
    tiles = sky_ref.shape[2] // SIDE
    for field in range(3):
        for t in range(tiles):
            slab_out[t // 8, field, :, t % 8, :] = sky_ref[field, :, t * SIDE:(t + 1) * SIDE]
    pl.semaphore_wait(barrier, groups - 1)

    def slab_copy(field, q, src_row):
        return send_row(
            q, slab_out.at[row_at[q], field], slab_in.at[src_row, field],
            (slab_sem.at[0, field, q], slab_sem.at[1, field, q]),
        )

    def own_slab(field):
        return pltpu.make_async_copy(
            slab_out.at[my_r, field], slab_in.at[my_r, field], self_sem.at[field]
        )

    for field in range(3):
        each_row_peer(lambda q: slab_copy(field, q, my_r).start())
        own_slab(field).start()

    low_index = lax.broadcasted_iota(jnp.int32, (SIDE, SIDE), 0)
    high_index = lax.broadcasted_iota(jnp.int32, (SIDE, SIDE), 1)
    column_ids = low_index + SIDE * high_index
    freq_cols = jnp.where(column_ids < NC // 2, column_ids, column_ids - NC)

    def row_frequency(row):
        row_id = me * local_rows + row
        return jnp.where(row_id < total_rows // 2, row_id, row_id - total_rows)

    def weigh(row, carry):
        scaled = row_ratio * row_frequency(row)
        radius_sq = freq_cols * freq_cols + scaled * scaled

        def mask(n):
            low, high = cuts_ref[2 * n], cuts_ref[2 * n + 1]
            inside = (radius_sq >= low * low) & (radius_sq <= high * high)
            return inside.astype(jnp.float32)

        pol = mask(1)
        weights[0, row] = mask(0) * weight_ref[0, row].T
        weights[1, row] = pol * weight_ref[1, row].T
        weights[2, row] = pol * weight_ref[2, row].T
        weights[3, row] = weight_ref[3, row].T
        weights[4, row] = weight_ref[4, row].T
        weights[5, row] = mask(2) * weight_ref[5, row].T
        return carry


    def spec_copy(field, row, q, src_block):
        return send(
            q, spec_out.at[field, row, peer_of(q)], spec_in.at[field, row, :, src_block],
            (spec_sem.at[0, field, row, q], spec_sem.at[1, field, row, q]),
        )

    def own_spec(field, row):
        return pltpu.make_async_copy(
            spec_out.at[field, row, me], spec_in.at[field, row, :, my_block],
            self_sem.at[3 + field * local_rows + row],
        )

    def spec_start(field, row):
        each_peer(lambda q: spec_copy(field, row, q, my_block).start())
        own_spec(field, row).start()

    def row_step(field, carry):
        each_row_peer(
            lambda q: slab_copy(field, q, row_at[rows_count - q]).wait_recv()
        )
        own_slab(field).wait()
        values = [
            (slab_in[y // in_rows, field, y % in_rows], None) for y in range(total_rows)
        ]
        for k, (real, imag) in enumerate(short_transform(values, -1)):
            spec_out[field, k % local_rows, k // local_rows, 0] = real
            spec_out[field, k % local_rows, k // local_rows, 1] = (
                jnp.zeros_like(real) if imag is None else imag
            )
        spec_start(field, 0)
        return carry

    lax.fori_loop(0, 3, row_step, 0)

    def later_rows(n, carry):
        spec_start(n % 3, 1 + n // 3)
        return carry

    lax.fori_loop(0, 3 * (local_rows - 1), later_rows, 0)

    def spec_wait(row):
        def step(field, carry):
            each_peer(lambda q: spec_copy(field, row, q, source_block(q)).wait_recv())
            own_spec(field, row).wait()
            return carry

        lax.fori_loop(0, 3, step, 0)

    cos_f, sin_f, cos_b, sin_b = 0, 1, 2, 3

    def side_by_side(pieces, axis):
        return pieces[0] if len(pieces) == 1 else jnp.concatenate(pieces, axis=axis)

    def long_forward(pieces):
        y = matrix_left(table_ref, 0, side_by_side(pieces, 1))
        c, s = twiddle_ref[cos_f], twiddle_ref[sin_f]
        turned = []
        for n in range(len(pieces)):
            yr, yi = y[:SIDE, n * SIDE:(n + 1) * SIDE], y[SIDE:, n * SIDE:(n + 1) * SIDE]
            turned.append(jnp.concatenate([yr * c - yi * s, yr * s + yi * c], axis=1))
        z = matrix_right(table_ref, 1, side_by_side(turned, 0))
        return [
            (z[n * SIDE:(n + 1) * SIDE, :SIDE], z[n * SIDE:(n + 1) * SIDE, SIDE:])
            for n in range(len(pieces))
        ]

    def long_inverse(pairs):
        stacks = [jnp.concatenate([pair[0], pair[1]], axis=1) for pair in pairs]
        u = matrix_right(table_ref, 0, side_by_side(stacks, 0))
        c, s = twiddle_ref[cos_b], twiddle_ref[sin_b]
        turned = []
        for n in range(len(pairs)):
            ur, ui = u[n * SIDE:(n + 1) * SIDE, :SIDE], u[n * SIDE:(n + 1) * SIDE, SIDE:]
            turned.append(jnp.concatenate([ur * c - ui * s, ur * s + ui * c], axis=0))
        x = matrix_left(table_ref, 1, side_by_side(turned, 1))
        return [
            x[:, n * SIDE:(n + 1) * SIDE].reshape((2, groups) + TILE)
            for n in range(len(pairs))
        ]

    leg_self = 3 + 3 * local_rows

    def legs_copy(row, g, q, src_index):
        first, count = LEG_GROUPS[g]
        return send(
            q, legs_out.at[row, first:first + count, :, peer_block(q)],
            legs_in.at[row, src_index, first:first + count],
            (legs_sem.at[0, row, g, q], legs_sem.at[1, row, g, q]),
        )

    def own_legs(row, g):
        first, count = LEG_GROUPS[g]
        return pltpu.make_async_copy(
            legs_out.at[row, first:first + count, :, my_block],
            legs_in.at[row, me, first:first + count],
            self_sem.at[leg_self + row * len(LEG_GROUPS) + g],
        )

    def slopes(row):
        along_x = (2 * freq_cols).astype(jnp.float32) / NC
        along_y = (2 * row_frequency(row)).astype(jnp.float32) / total_rows
        return along_x, along_y

    def leg_step(row, carry):
        spec_wait(row)
        temp, stokes_q, stokes_u = long_forward(
            [spec_in[field, row].reshape(2 * SIDE, SIDE) for field in range(3)]
        )
        scaled = row_ratio * row_frequency(row)
        radius_sq = freq_cols * freq_cols + scaled * scaled
        floor = jnp.maximum(radius_sq, 1).astype(jnp.float32)
        cos2 = (freq_cols * freq_cols - scaled * scaled).astype(jnp.float32) / floor
        sin2 = (2 * freq_cols * scaled).astype(jnp.float32) / floor
        along_x, along_y = slopes(row)
        raising, lowering = (-along_y, along_x), (along_y, along_x)
        rot = (cos2, sin2)
        w_t, w_e, w_b = weights[0, row], weights[1, row], weights[2, row]
        w_gt, w_ge = weights[3, row], weights[4, row]
        t_bar = (w_t * temp[0], w_t * temp[1])
        e_bar = tuple(-w_e * (cos2 * a + sin2 * b) for a, b in zip(stokes_q, stokes_u))
        b_bar = tuple(w_b * (sin2 * a - cos2 * b) for a, b in zip(stokes_q, stokes_u))
        g = complex_mul((w_gt * t_bar[0], w_gt * t_bar[1]), raising)
        p = complex_mul((b_bar[1] - e_bar[0], -(e_bar[1] + b_bar[0])), rot)
        w = complex_mul((-w_ge * e_bar[0], -w_ge * e_bar[1]), rot)
        h3 = complex_mul(w, raising)
        h1 = complex_mul(w, lowering)
        legs = (t_bar, g, p, h3, h1)
        for n, (first, count) in enumerate(LEG_GROUPS):
            for k, leg_map in enumerate(long_inverse(legs[first:first + count])):
                legs_out[row, first + k] = leg_map
            each_peer(lambda q: legs_copy(row, n, q, me).start())
            own_legs(row, n).start()
        return carry

    for load in loads[1:]:
        load.wait()

    def spread(n, carry):
        for j in range(8):
            start = pl.multiple_of((n * 8 + j) * SIDE, SIDE)
            weight_ref[:, :, n * 8 + j, :] = raw[:, :, pl.ds(start, SIDE)]
        return carry

    lax.fori_loop(0, SIDE // 8, spread, 0)
    lax.fori_loop(0, local_rows, weigh, 0)
    lax.fori_loop(0, local_rows, leg_step, 0)

    for field in range(3):
        each_row_peer(lambda q: slab_copy(field, q, my_r).wait_send())

    def spec_left(n, carry):
        each_peer(lambda q: spec_copy(n % 3, n // 3, q, my_block).wait_send())
        return carry

    lax.fori_loop(0, 3 * local_rows, spec_left, 0)

    def leg_wait(g):
        def step(row, carry):
            each_peer(lambda q: legs_copy(row, g, q, source_of(q)).wait_recv())
            own_legs(row, g).wait()
            return carry

        lax.fori_loop(0, local_rows, step, 0)

    def map_step(n, carry):
        values = [
            (legs_in[k % local_rows, k // local_rows, n, 0],
             legs_in[k % local_rows, k // local_rows, n, 1])
            for k in range(total_rows)
        ]
        for y, (real, imag) in enumerate(short_transform(values, 1)):
            maps[n, 0, y] = real
            maps[n, 1, y] = imag
        return carry

    for g, (first, count) in enumerate(LEG_GROUPS):
        leg_wait(g)
        lax.fori_loop(first, first + count, map_step, 0)

    def product_step(y, carry):
        a, g, p, h3, h1 = [(maps[n, 0, y], maps[n, 1, y]) for n in range(5)]
        ag, ph, hp = complex_mul(a, g), conj_mul(p, h3), conj_mul(h1, p)
        current[0, y] = ag[0] + 0.5 * (ph[0] + hp[0])
        current[1, y] = ag[1] + 0.5 * (ph[1] + hp[1])
        return carry

    lax.fori_loop(0, total_rows, product_step, 0)

    values = [(current[0, y], current[1, y]) for y in range(total_rows)]
    for k, (real, imag) in enumerate(short_transform(values, -1)):
        cur_out[k % local_rows, k // local_rows, 0] = real
        cur_out[k % local_rows, k // local_rows, 1] = imag
    cur_self = leg_self + len(LEG_GROUPS) * local_rows
    est_self = cur_self + local_rows

    def cur_copy(row, q, src_block):
        return send(
            q, cur_out.at[row, peer_of(q)], cur_in.at[row, :, src_block],
            (cur_sem.at[0, row, q], cur_sem.at[1, row, q]),
        )

    def own_cur(row):
        return pltpu.make_async_copy(
            cur_out.at[row, me], cur_in.at[row, :, my_block], self_sem.at[cur_self + row]
        )

    def cur_start(row, carry):
        each_peer(lambda q: cur_copy(row, q, my_block).start())
        own_cur(row).start()
        return carry

    lax.fori_loop(0, local_rows, cur_start, 0)

    def legs_left(row, carry):
        for g in range(len(LEG_GROUPS)):
            each_peer(lambda q: legs_copy(row, g, q, me).wait_send())
        return carry

    lax.fori_loop(0, local_rows, legs_left, 0)

    def est_copy(row, q, src_index):
        return send(
            q, est_out.at[row, :, peer_block(q)], est_in.at[row, src_index],
            (est_sem.at[0, row, q], est_sem.at[1, row, q]),
        )

    def own_est(row):
        return pltpu.make_async_copy(
            est_out.at[row, :, my_block], est_in.at[row, me], self_sem.at[est_self + row]
        )

    def estimate_step(row, carry):
        each_peer(lambda q: cur_copy(row, q, source_block(q)).wait_recv())
        own_cur(row).wait()
        (modes,) = long_forward([cur_in[row].reshape(2 * SIDE, SIDE)])
        along_x, along_y = slopes(row)
        w = weights[5, row]
        estimate = complex_mul((w * modes[0], w * modes[1]), (along_y, along_x))
        (est_out[row],) = long_inverse([estimate])
        each_peer(lambda q: est_copy(row, q, me).start())
        own_est(row).start()
        return carry

    lax.fori_loop(0, local_rows, estimate_step, 0)

    def cur_left(row, carry):
        each_peer(lambda q: cur_copy(row, q, my_block).wait_send())
        return carry

    lax.fori_loop(0, local_rows, cur_left, 0)

    def est_wait(row, carry):
        each_peer(lambda q: est_copy(row, q, source_of(q)).wait_recv())
        own_est(row).wait()
        return carry

    lax.fori_loop(0, local_rows, est_wait, 0)

    values = [
        (est_in[k % local_rows, k // local_rows, 0], est_in[k % local_rows, k // local_rows, 1])
        for k in range(total_rows)
    ]
    for y, (real, imag) in enumerate(short_transform(values, 1)):
        fin_out[y // in_rows, 0, y % in_rows] = real
        fin_out[y // in_rows, 1, y % in_rows] = imag

    def fin_copy(q, src_row):
        return send_row(
            q, fin_out.at[row_at[q]], fin_in.at[src_row],
            (fin_sem.at[0, q], fin_sem.at[1, q]),
        )

    each_row_peer(lambda q: fin_copy(q, my_r).start())
    own_fin = pltpu.make_async_copy(
        fin_out.at[my_r], fin_in.at[my_r], self_sem.at[est_self + local_rows]
    )
    own_fin.start()

    def est_left(row, carry):
        each_peer(lambda q: est_copy(row, q, me).wait_send())
        return carry

    lax.fori_loop(0, local_rows, est_left, 0)
    each_row_peer(lambda q: fin_copy(q, row_at[rows_count - q]).wait_recv())
    own_fin.wait()
    for part in range(2):
        for t in range(tiles):
            out_ref[part, :, t * SIDE:(t + 1) * SIDE] = fin_in[t // 8, part, :, t % 8, :]

    each_row_peer(lambda q: fin_copy(q, my_r).wait_send())


def long_tables(total_rows):
    index = np.arange(SIDE)
    angle = 2.0 * np.pi * (index[:, None] * index[None, :] % SIDE) / SIDE
    c, s = np.cos(angle), np.sin(angle)
    forward = np.block([[c, s], [-s, c]]).astype(np.float32)
    tables = np.stack([forward, forward.T])
    top = tables.astype(jnp.bfloat16)
    rest = (tables - top.astype(np.float32)).astype(jnp.bfloat16)
    turn = 2.0 * np.pi * (index[:, None] * index[None, :]) / NC
    scale = 1.0 / (NC * total_rows)
    twiddle = np.stack(
        [np.cos(turn), -np.sin(turn), scale * np.cos(turn), scale * np.sin(turn)]
    ).astype(np.float32)
    return np.stack([top, rest], axis=1), twiddle


def fused_body(rows_count, fields_count, sky_maps, band_cuts, filters, wiener, response):
    groups = rows_count * fields_count
    local_rows = response.shape[0]
    total_rows = local_rows * groups
    in_rows = total_rows // rows_count
    table, twiddle = long_tables(total_rows)
    vmem = pl.BlockSpec(memory_space=pltpu.VMEM)
    f32 = jnp.float32
    dma = pltpu.SemaphoreType.DMA
    slab = pltpu.VMEM((rows_count, 3, in_rows) + TILE, f32)
    chunk = pltpu.VMEM((local_rows, groups, 2) + TILE, f32)
    lines = pltpu.VMEM((local_rows, 2, groups) + TILE, f32)
    final = pltpu.VMEM((rows_count, 2, in_rows) + TILE, f32)
    return pl.pallas_call(
        functools.partial(lens_kernel, rows_count, fields_count, local_rows),
        out_shape=jax.ShapeDtypeStruct((2,) + sky_maps.shape[1:], f32),
        in_specs=[pl.BlockSpec(memory_space=pltpu.SMEM)]
        + [pl.BlockSpec(memory_space=pl.ANY)] * 4
        + [vmem] * 2,
        out_specs=vmem,
        scratch_shapes=[
            pltpu.VMEM(sky_maps.shape, f32),
            pltpu.VMEM((6, local_rows, NC), f32),
            pltpu.VMEM((6, local_rows, SIDE, SIDE), f32),
            slab, slab,
            pltpu.VMEM((3, local_rows, groups, 2) + TILE, f32),
            pltpu.VMEM((3, local_rows, 2, groups) + TILE, f32),
            pltpu.VMEM((6, local_rows, SIDE, SIDE), f32),
            pltpu.VMEM((local_rows, 5, 2, groups) + TILE, f32),
            pltpu.VMEM((local_rows, groups, 5, 2) + TILE, f32),
            pltpu.VMEM((5, 2, total_rows) + TILE, f32),
            pltpu.VMEM((2, total_rows) + TILE, f32),
            chunk, lines, lines, chunk, final, final,
            dma((2, 3, rows_count)), dma((2, 3, local_rows, groups - 1)),
            dma((2, local_rows, len(LEG_GROUPS), groups - 1)),
            dma((2, local_rows, groups - 1)), dma((2, local_rows, groups - 1)),
            dma((2, rows_count)), dma((4 + (5 + len(LEG_GROUPS)) * local_rows,)),
            dma((4,)),
        ],
        compiler_params=pltpu.CompilerParams(
            collective_id=0, has_side_effects=True, vmem_limit_bytes=60 * 1024 * 1024
        ),
        name="lens",
    )(band_cuts, sky_maps, filters, wiener, response, jnp.asarray(table), jnp.asarray(twiddle))


def solution(mesh):
    placed = (
        P("sims", "rows", "fields"),
        P(),
        P(None, ("rows", "fields"), None),
        P(None, ("rows", "fields"), None),
        P(("rows", "fields"), None),
    )
    rows_count, fields_count = mesh.shape["rows"], mesh.shape["fields"]
    groups = rows_count * fields_count

    def choose(sky_maps, *rest):
        fits = (
            NC == SIDE * SIDE
            and fields_count % 2 == 0
            and NC // groups == TILE[0] * TILE[1]
            and sky_maps.shape[1] % 8 == 0
            and sky_maps.shape[1] * rows_count in (16, 32, 64)
        )
        if fits:
            return fused_body(rows_count, fields_count, sky_maps, *rest)
        return body(sky_maps, *rest)

    return jax.shard_map(
        choose, mesh=mesh, in_specs=placed, out_specs=P("sims", "rows", "fields"), check_vma=False
    )
```

profile of v0, /device:TPU:3, one launch (start us, length us, event | category | flops | bytes accessed | tf_op | source)
XLA Modules:
  0.0 83.4 jit_solution(115117369393550211)
XLA Ops:
  0.0 81.7 %lens.1 = f32[2,8,4096]{2,1,0:T(8,128)} custom-call(s32[6]{0:T(128)} %cuts_ref.1, f32[3,8,4096]{2,1,0:T(8,128)} %sky_hbm.1, f32[3,2,16384]{2,1,0:T(2,128)} %filters_hbm.1, f32[2,2,16384]{2,1,0:T(2,128)} %wiener_hbm.1, f32[2,16384]{1,0:T(2,128)} %response_hbm.1, bf16[2,2,256,256]{3,2,1,0:T(8,128)(2,1)} %constant.4.clone.table_ref, ...), custom_call_target="tpu_custom_call" | custom-call | tf_op jit(solution)/shard_map/lens/pallas_call | solution.py:799
  81.7 1.7 %copy.9 = f32[2,8,4096]{2,1,0:T(8,128)} copy(f32[2,8,4096]{2,1,0:T(8,128)} %lens.1) | data formatting | bytes 524288
where the time goes:
time: 84.4 us; the launch traced here: 83.4 us
  Pallas kernels  81.7 us (97%)
  local copies, waits for them, and re-layouts  1.67 us (2%)
    pallas_call x1, Pallas kernels, fused_body(): pl.pallas_call(functools.partial(lens_kernel, rows_count, fields_count, l...  81.7 us

commit v1 on v0

--- a/solution.py
+++ b/solution.py
@@ -335,75 +335,60 @@
     return dot32(top, m_top) + (dot32(top, m_rest) + dot32(rest, m_top))
 
 
+BITS = (0, 1)
+OFFSETS = [
+    (c, a1, e, a0) for a0 in BITS for c, a1, e in
+    ((1, 1, 1), (1, 0, 0), (0, 1, 0), (0, 0, 1), (1, 1, 0), (0, 1, 1), (1, 0, 1), (0, 0, 0))
+]
+PEERS = [offset for offset in OFFSETS if any(offset)]
+WEIGHT_ORDER = (0, 3, 1, 2, 4, 5)
+
+
 def lens_kernel(
-    rows_count, fields_count, local_rows,
     cuts_ref, sky_hbm, filters_hbm, wiener_hbm, response_hbm, table_ref, twiddle_ref, out_ref,
-    sky_ref, raw, weight_ref, slab_out, slab_in, spec_out, spec_in, weights, legs_out, legs_in, maps, current,
-    cur_out, cur_in, est_out, est_in, fin_out, fin_in,
-    slab_sem, spec_sem, legs_sem, cur_sem, est_sem, fin_sem, self_sem, load_sem,
+    sky_ref, raw, weight_ref, slab_out, slab_in, relay_buf, spec_out, spec_in, weights, legs_out, legs_in,
+    maps, current, cur_out, cur_in, est_out, est_in, fin_out, fin_in,
+    slab_sem, relay_sem, forward_sem, spec_sem, weight_sem, legs_sem, cur_sem, est_sem, fin_sem, self_sem, load_sem,
 ):
+    rows_count, fields_count, local_rows = 4, 4, 2
     groups = rows_count * fields_count
     total_rows = groups * local_rows
     in_rows = total_rows // rows_count
     row_ratio = NC // total_rows
-    my_r, my_f = lax.axis_index("rows"), lax.axis_index("fields")
-    me = my_r * fields_count + my_f
-    my_block = my_f * rows_count + my_r
-
-    half = fields_count // 2
-    my_half, my_spot = my_f // half, my_f % half
-
-    def wrapped(value, length):
-        return jnp.where(value >= length, value - length, value)
-
-    row_at = [wrapped(my_r + d, rows_count) for d in range(rows_count)]
-    spot_at = [wrapped(my_spot + d, half) for d in range(half)]
-    side_at = [my_half * half, (1 - my_half) * half]
-
-    def partner(q, sign):
-        side = 1 - q // (rows_count * half)
-        spot = sign * (q // rows_count + 1) % half
-        return row_at[sign * (q + 1) % rows_count], side_at[side] + spot_at[spot]
-
-    def peer_of(q):
-        r, f = partner(q, 1)
-        return r * fields_count + f
-
-    def source_of(q):
-        r, f = partner(q, -1)
-        return r * fields_count + f
-
-    def peer_block(q):
-        r, f = partner(q, 1)
-        return f * rows_count + r
-
-    def source_block(q):
-        r, f = partner(q, -1)
-        return f * rows_count + r
-
-    def target(q):
-        r, f = partner(q, 1)
-        return {"rows": r, "fields": f}
-
-    def send(q, src, dst, sems):
+    my_x, my_r, my_z = (lax.axis_index(name) for name in ("sims", "rows", "fields"))
+    my_y, my_c, my_h, my_l = my_r // 2, my_r % 2, my_z // 2, my_z % 2
+    x_at, y_at, c_at, h_at, l_at = ((bit, 1 - bit) for bit in (my_x, my_y, my_c, my_h, my_l))
+    me = my_r * fields_count + 2 * my_x + my_l
+    my_block = (2 * my_x + my_l) * rows_count + my_r
+    stays = my_x == my_h
+
+    def row_of(offset):
+        return 2 * y_at[offset[1]] + c_at[offset[3]]
+
+    def peer_of(offset):
+        return row_of(offset) * fields_count + 2 * x_at[offset[0]] + l_at[offset[2]]
+
+    def peer_block(offset):
+        return (2 * x_at[offset[0]] + l_at[offset[2]]) * rows_count + row_of(offset)
+
+    def home_source(offset):
+        return row_of(offset) * fields_count + 2 * h_at[offset[0]] + l_at[offset[2]]
+
+    def remote(src, dst, sems, x, r, z):
         return pltpu.make_async_remote_copy(
             src_ref=src, dst_ref=dst, send_sem=sems[0], recv_sem=sems[1],
-            device_id=target(q), device_id_type=MESH,
-        )
-
-    def send_row(q, src, dst, sems):
-        return pltpu.make_async_remote_copy(
-            src_ref=src, dst_ref=dst, send_sem=sems[0], recv_sem=sems[1],
-            device_id={"rows": row_at[q]}, device_id_type=MESH,
-        )
+            device_id={"sims": x, "rows": r, "fields": z}, device_id_type=MESH,
+        )
+
+    def send(offset, src, dst, sems):
+        return remote(src, dst, sems, x_at[offset[0]], row_of(offset), 2 * my_h + l_at[offset[2]])
+
+    def send_home(offset, src, dst, sems):
+        return remote(src, dst, sems, my_h, row_of(offset), 2 * x_at[offset[0]] + l_at[offset[2]])
 
     def each_peer(body):
-        for q in range(groups - 1):
-            body(q)
-
-    def each_row_peer(body):
-        for q in range(1, rows_count):
-            body(q)
+        for q, offset in enumerate(PEERS):
+            body(q, offset)
 
     loads = [
         pltpu.make_async_copy(src, dst, load_sem.at[n])
@@ -418,34 +403,59 @@
         load.start()
 
     barrier = pltpu.get_barrier_semaphore()
-
-    def greet(q):
-        pl.semaphore_signal(
-            barrier, inc=1, device_id=target(q), device_id_type=MESH
-        )
-
-    each_peer(greet)
+    for h in BITS:
+        for c, a1, e, a0 in OFFSETS:
+            if h or c or a1 or e or a0:
+                pl.semaphore_signal(
+                    barrier, inc=1, device_id_type=MESH,
+                    device_id={"sims": x_at[c], "rows": 2 * y_at[a1] + c_at[a0], "fields": 2 * h_at[h] + l_at[e]},
+                )
     loads[0].wait()
     tiles = sky_ref.shape[2] // SIDE
     for field in range(3):
         for t in range(tiles):
             slab_out[t // 8, field, :, t % 8, :] = sky_ref[field, :, t * SIDE:(t + 1) * SIDE]
-    pl.semaphore_wait(barrier, groups - 1)
-
-    def slab_copy(field, q, src_row):
-        return send_row(
-            q, slab_out.at[row_at[q], field], slab_in.at[src_row, field],
-            (slab_sem.at[0, field, q], slab_sem.at[1, field, q]),
+    pl.semaphore_wait(barrier, 2 * groups - 1)
+
+    ROW_OFFSETS = [(0, a1, 0, a0) for a1 in BITS for a0 in BITS]
+
+    def slab_copy(field, offset, source_row):
+        r = row_of(offset)
+        return send_home(
+            offset, slab_out.at[r, field], slab_in.at[source_row, field],
+            (slab_sem.at[0, field, 2 * offset[1] + offset[3]], slab_sem.at[1, field, 2 * offset[1] + offset[3]]),
         )
 
     def own_slab(field):
-        return pltpu.make_async_copy(
-            slab_out.at[my_r, field], slab_in.at[my_r, field], self_sem.at[field]
-        )
-
-    for field in range(3):
-        each_row_peer(lambda q: slab_copy(field, q, my_r).start())
-        own_slab(field).start()
+        return pltpu.make_async_copy(slab_out.at[my_r, field], slab_in.at[my_r, field], self_sem.at[field])
+
+    def relay_copy(field):
+        return remote(
+            slab_out.at[pl.ds(2 * y_at[1], 2), field], relay_buf.at[field],
+            (relay_sem.at[0, field], relay_sem.at[1, field]), x_at[1], my_r, my_z,
+        )
+
+    def forward_copy(field, core):
+        a0 = core
+        return remote(
+            relay_buf.at[field, c_at[a0]], slab_in.at[my_r, field],
+            (forward_sem.at[field, a0], slab_sem.at[1, field, 2 + a0]),
+            my_x, 2 * y_at[1] + c_at[a0], 2 * h_at[1] + my_l,
+        )
+
+    @pl.when(stays)
+    def _():
+        for field in range(3):
+            own_slab(field).start()
+            for offset in ROW_OFFSETS[1:]:
+                slab_copy(field, offset, my_r).start()
+
+    @pl.when(jnp.logical_not(stays))
+    def _():
+        for field in range(3):
+            relay_copy(field).start()
+            for offset in ROW_OFFSETS[:2]:
+                slab_copy(field, offset, my_r).start()
 
     low_index = lax.broadcasted_iota(jnp.int32, (SIDE, SIDE), 0)
     high_index = lax.broadcasted_iota(jnp.int32, (SIDE, SIDE), 1)
@@ -453,31 +463,18 @@
     freq_cols = jnp.where(column_ids < NC // 2, column_ids, column_ids - NC)
 
     def row_frequency(row):
-        row_id = me * local_rows + row
+        row_id = in_rows * my_r + 4 * (my_h + row - 2 * my_h * row) + 2 * my_l + my_x
         return jnp.where(row_id < total_rows // 2, row_id, row_id - total_rows)
 
-    def weigh(row, carry):
-        scaled = row_ratio * row_frequency(row)
-        radius_sq = freq_cols * freq_cols + scaled * scaled
-
-        def mask(n):
-            low, high = cuts_ref[2 * n], cuts_ref[2 * n + 1]
-            inside = (radius_sq >= low * low) & (radius_sq <= high * high)
-            return inside.astype(jnp.float32)
-
-        pol = mask(1)
-        weights[0, row] = mask(0) * weight_ref[0, row].T
-        weights[1, row] = pol * weight_ref[1, row].T
-        weights[2, row] = pol * weight_ref[2, row].T
-        weights[3, row] = weight_ref[3, row].T
-        weights[4, row] = weight_ref[4, row].T
-        weights[5, row] = mask(2) * weight_ref[5, row].T
-        return carry
-
-
-    def spec_copy(field, row, q, src_block):
+    def owner(k):
+        return k // 8 * fields_count + 2 * (k % 2) + k // 2 % 2
+
+    def local_row(k, half):
+        return 1 - half if k // 4 % 2 else half
+
+    def spec_copy(field, row, q, offset, block):
         return send(
-            q, spec_out.at[field, row, peer_of(q)], spec_in.at[field, row, :, src_block],
+            offset, spec_out.at[field, row, peer_of(offset)], spec_in.at[field, row, :, block],
             (spec_sem.at[0, field, row, q], spec_sem.at[1, field, row, q]),
         )
 
@@ -488,20 +485,29 @@
         )
 
     def spec_start(field, row):
-        each_peer(lambda q: spec_copy(field, row, q, my_block).start())
+        each_peer(lambda q, offset: spec_copy(field, row, q, offset, my_block).start())
         own_spec(field, row).start()
 
     def row_step(field, carry):
-        each_row_peer(
-            lambda q: slab_copy(field, q, row_at[rows_count - q]).wait_recv()
-        )
-        own_slab(field).wait()
+        @pl.when(stays)
+        def _():
+            relay_copy(field).wait_recv()
+            for core in BITS:
+                forward_copy(field, core).start()
+            own_slab(field).wait()
+
+        @pl.when(jnp.logical_not(stays))
+        def _():
+            slab_copy(field, ROW_OFFSETS[0], my_r).wait_recv()
+
+        for offset in ROW_OFFSETS[1:]:
+            slab_copy(field, offset, row_of(offset)).wait_recv()
         values = [
             (slab_in[y // in_rows, field, y % in_rows], None) for y in range(total_rows)
         ]
         for k, (real, imag) in enumerate(short_transform(values, -1)):
-            spec_out[field, k % local_rows, k // local_rows, 0] = real
-            spec_out[field, k % local_rows, k // local_rows, 1] = (
+            spec_out[field, local_row(k, my_h), owner(k), 0] = real
+            spec_out[field, local_row(k, my_h), owner(k), 1] = (
                 jnp.zeros_like(real) if imag is None else imag
             )
         spec_start(field, 0)
@@ -509,15 +515,49 @@
 
     lax.fori_loop(0, 3, row_step, 0)
 
-    def later_rows(n, carry):
-        spec_start(n % 3, 1 + n // 3)
+    def later_rows(field, carry):
+        spec_start(field, 1)
         return carry
 
-    lax.fori_loop(0, 3 * (local_rows - 1), later_rows, 0)
+    lax.fori_loop(0, 3, later_rows, 0)
+
+    for load in loads[1:]:
+        load.wait()
+
+    def spread(n, carry):
+        for j in range(8):
+            start = pl.multiple_of((n * 8 + j) * SIDE, SIDE)
+            weight_ref[:, :, n * 8 + j, :] = raw[:, :, pl.ds(start, SIDE)]
+        return carry
+
+    lax.fori_loop(0, SIDE // 8, spread, 0)
+    scaled_home = row_ratio * row_frequency(0)
+    radius_home = freq_cols * freq_cols + scaled_home * scaled_home
+
+    def mask(n):
+        low, high = cuts_ref[2 * n], cuts_ref[2 * n + 1]
+        inside = (radius_home >= low * low) & (radius_home <= high * high)
+        return inside.astype(jnp.float32)
+
+    def weight_copy(n):
+        return remote(
+            weights.at[n, 0], weights.at[n, 1], (weight_sem.at[0, n], weight_sem.at[1, n]),
+            my_x, my_r, 2 * h_at[1] + my_l,
+        )
+
+    pol = mask(1)
+    weights[0, 0] = mask(0) * weight_ref[0, my_x].T
+    weights[1, 0] = pol * weight_ref[1, my_x].T
+    weights[2, 0] = pol * weight_ref[2, my_x].T
+    weights[3, 0] = weight_ref[3, my_x].T
+    weights[4, 0] = weight_ref[4, my_x].T
+    weights[5, 0] = mask(2) * weight_ref[5, my_x].T
+    for n in WEIGHT_ORDER:
+        weight_copy(n).start()
 
     def spec_wait(row):
         def step(field, carry):
-            each_peer(lambda q: spec_copy(field, row, q, source_block(q)).wait_recv())
+            each_peer(lambda q, offset: spec_copy(field, row, q, offset, peer_block(offset)).wait_recv())
             own_spec(field, row).wait()
             return carry
 
@@ -557,11 +597,11 @@
 
     leg_self = 3 + 3 * local_rows
 
-    def legs_copy(row, g, q, src_index):
+    def legs_copy(row, g, q, offset, source):
         first, count = LEG_GROUPS[g]
         return send(
-            q, legs_out.at[row, first:first + count, :, peer_block(q)],
-            legs_in.at[row, src_index, first:first + count],
+            offset, legs_out.at[row, first:first + count, :, peer_block(offset)],
+            legs_in.at[row, source, first:first + count],
             (legs_sem.at[0, row, g, q], legs_sem.at[1, row, g, q]),
         )
 
@@ -580,6 +620,12 @@
 
     def leg_step(row, carry):
         spec_wait(row)
+
+        @pl.when(row == 1)
+        def _():
+            for n in WEIGHT_ORDER[:5]:
+                weight_copy(n).wait_recv()
+
         temp, stokes_q, stokes_u = long_forward(
             [spec_in[field, row].reshape(2 * SIDE, SIDE) for field in range(3)]
         )
@@ -605,35 +651,15 @@
         for n, (first, count) in enumerate(LEG_GROUPS):
             for k, leg_map in enumerate(long_inverse(legs[first:first + count])):
                 legs_out[row, first + k] = leg_map
-            each_peer(lambda q: legs_copy(row, n, q, me).start())
+            each_peer(lambda q, offset: legs_copy(row, n, q, offset, me).start())
             own_legs(row, n).start()
         return carry
 
-    for load in loads[1:]:
-        load.wait()
-
-    def spread(n, carry):
-        for j in range(8):
-            start = pl.multiple_of((n * 8 + j) * SIDE, SIDE)
-            weight_ref[:, :, n * 8 + j, :] = raw[:, :, pl.ds(start, SIDE)]
-        return carry
-
-    lax.fori_loop(0, SIDE // 8, spread, 0)
-    lax.fori_loop(0, local_rows, weigh, 0)
     lax.fori_loop(0, local_rows, leg_step, 0)
-
-    for field in range(3):
-        each_row_peer(lambda q: slab_copy(field, q, my_r).wait_send())
-
-    def spec_left(n, carry):
-        each_peer(lambda q: spec_copy(n % 3, n // 3, q, my_block).wait_send())
-        return carry
-
-    lax.fori_loop(0, 3 * local_rows, spec_left, 0)
 
     def leg_wait(g):
         def step(row, carry):
-            each_peer(lambda q: legs_copy(row, g, q, source_of(q)).wait_recv())
+            each_peer(lambda q, offset: legs_copy(row, g, q, offset, peer_of(offset)).wait_recv())
             own_legs(row, g).wait()
             return carry
 
@@ -641,8 +667,7 @@
 
     def map_step(n, carry):
         values = [
-            (legs_in[k % local_rows, k // local_rows, n, 0],
-             legs_in[k % local_rows, k // local_rows, n, 1])
+            (legs_in[local_row(k, my_h), owner(k), n, 0], legs_in[local_row(k, my_h), owner(k), n, 1])
             for k in range(total_rows)
         ]
         for y, (real, imag) in enumerate(short_transform(values, 1)):
@@ -665,14 +690,14 @@
 
     values = [(current[0, y], current[1, y]) for y in range(total_rows)]
     for k, (real, imag) in enumerate(short_transform(values, -1)):
-        cur_out[k % local_rows, k // local_rows, 0] = real
-        cur_out[k % local_rows, k // local_rows, 1] = imag
+        cur_out[local_row(k, my_h), owner(k), 0] = real
+        cur_out[local_row(k, my_h), owner(k), 1] = imag
     cur_self = leg_self + len(LEG_GROUPS) * local_rows
     est_self = cur_self + local_rows
 
-    def cur_copy(row, q, src_block):
+    def cur_copy(row, q, offset, block):
         return send(
-            q, cur_out.at[row, peer_of(q)], cur_in.at[row, :, src_block],
+            offset, cur_out.at[row, peer_of(offset)], cur_in.at[row, :, block],
             (cur_sem.at[0, row, q], cur_sem.at[1, row, q]),
         )
 
@@ -682,24 +707,19 @@
         )
 
     def cur_start(row, carry):
-        each_peer(lambda q: cur_copy(row, q, my_block).start())
+        each_peer(lambda q, offset: cur_copy(row, q, offset, my_block).start())
         own_cur(row).start()
         return carry
 
     lax.fori_loop(0, local_rows, cur_start, 0)
 
-    def legs_left(row, carry):
-        for g in range(len(LEG_GROUPS)):
-            each_peer(lambda q: legs_copy(row, g, q, me).wait_send())
-        return carry
-
-    lax.fori_loop(0, local_rows, legs_left, 0)
-
-    def est_copy(row, q, src_index):
-        return send(
-            q, est_out.at[row, :, peer_block(q)], est_in.at[row, src_index],
+    def est_copy(row, q, offset, source):
+        return send_home(
+            offset, est_out.at[row, :, peer_block(offset)], est_in.at[row, source],
             (est_sem.at[0, row, q], est_sem.at[1, row, q]),
         )
+
+    ORIGIN = (0, 0, 0, 0)
 
     def own_est(row):
         return pltpu.make_async_copy(
@@ -707,64 +727,110 @@
         )
 
     def estimate_step(row, carry):
-        each_peer(lambda q: cur_copy(row, q, source_block(q)).wait_recv())
+        each_peer(lambda q, offset: cur_copy(row, q, offset, peer_block(offset)).wait_recv())
         own_cur(row).wait()
+
+        @pl.when(row == 1)
+        def _():
+            weight_copy(5).wait_recv()
+
         (modes,) = long_forward([cur_in[row].reshape(2 * SIDE, SIDE)])
         along_x, along_y = slopes(row)
         w = weights[5, row]
         estimate = complex_mul((w * modes[0], w * modes[1]), (along_y, along_x))
         (est_out[row],) = long_inverse([estimate])
-        each_peer(lambda q: est_copy(row, q, me).start())
-        own_est(row).start()
+        each_peer(lambda q, offset: est_copy(row, q, offset, me).start())
+
+        @pl.when(stays)
+        def _():
+            own_est(row).start()
+
+        @pl.when(jnp.logical_not(stays))
+        def _():
+            est_copy(row, groups - 1, ORIGIN, me).start()
+
         return carry
 
     lax.fori_loop(0, local_rows, estimate_step, 0)
 
-    def cur_left(row, carry):
-        each_peer(lambda q: cur_copy(row, q, my_block).wait_send())
+    def est_wait(row, carry):
+        each_peer(lambda q, offset: est_copy(row, q, offset, home_source(offset)).wait_recv())
+
+        @pl.when(stays)
+        def _():
+            own_est(row).wait()
+
+        @pl.when(jnp.logical_not(stays))
+        def _():
+            est_copy(row, groups - 1, ORIGIN, home_source(ORIGIN)).wait_recv()
+
         return carry
 
-    lax.fori_loop(0, local_rows, cur_left, 0)
-
-    def est_wait(row, carry):
-        each_peer(lambda q: est_copy(row, q, source_of(q)).wait_recv())
-        own_est(row).wait()
-        return carry
-
     lax.fori_loop(0, local_rows, est_wait, 0)
 
     values = [
-        (est_in[k % local_rows, k // local_rows, 0], est_in[k % local_rows, k // local_rows, 1])
+        (est_in[local_row(k, my_x), owner(k), 0], est_in[local_row(k, my_x), owner(k), 1])
         for k in range(total_rows)
     ]
     for y, (real, imag) in enumerate(short_transform(values, 1)):
         fin_out[y // in_rows, 0, y % in_rows] = real
         fin_out[y // in_rows, 1, y % in_rows] = imag
 
-    def fin_copy(q, src_row):
-        return send_row(
-            q, fin_out.at[row_at[q]], fin_in.at[src_row],
-            (fin_sem.at[0, q], fin_sem.at[1, q]),
-        )
-
-    each_row_peer(lambda q: fin_copy(q, my_r).start())
+    def fin_copy(q, offset, source_row):
+        r = row_of(offset)
+        return remote(
+            fin_out.at[r], fin_in.at[source_row], (fin_sem.at[0, q], fin_sem.at[1, q]), my_x, r, my_z
+        )
+
+    for q, offset in enumerate(ROW_OFFSETS[1:]):
+        fin_copy(q, offset, my_r).start()
     own_fin = pltpu.make_async_copy(
         fin_out.at[my_r], fin_in.at[my_r], self_sem.at[est_self + local_rows]
     )
     own_fin.start()
 
-    def est_left(row, carry):
-        each_peer(lambda q: est_copy(row, q, me).wait_send())
+    @pl.when(stays)
+    def _():
+        for field in range(3):
+            for offset in ROW_OFFSETS[1:]:
+                slab_copy(field, offset, my_r).wait_send()
+            for core in BITS:
+                forward_copy(field, core).wait_send()
+
+    @pl.when(jnp.logical_not(stays))
+    def _():
+        for field in range(3):
+            relay_copy(field).wait_send()
+            for offset in ROW_OFFSETS[:2]:
+                slab_copy(field, offset, my_r).wait_send()
+        for row in range(local_rows):
+            est_copy(row, groups - 1, ORIGIN, me).wait_send()
+
+    for n in WEIGHT_ORDER:
+        weight_copy(n).wait_send()
+
+    def sends_left(row, carry):
+        def spec_left(field, inner):
+            each_peer(lambda q, offset: spec_copy(field, row, q, offset, my_block).wait_send())
+            return inner
+
+        lax.fori_loop(0, 3, spec_left, 0)
+        for g in range(len(LEG_GROUPS)):
+            each_peer(lambda q, offset: legs_copy(row, g, q, offset, me).wait_send())
+        each_peer(lambda q, offset: cur_copy(row, q, offset, my_block).wait_send())
+        each_peer(lambda q, offset: est_copy(row, q, offset, me).wait_send())
         return carry
 
-    lax.fori_loop(0, local_rows, est_left, 0)
-    each_row_peer(lambda q: fin_copy(q, row_at[rows_count - q]).wait_recv())
+    lax.fori_loop(0, local_rows, sends_left, 0)
+    for q, offset in enumerate(ROW_OFFSETS[1:]):
+        fin_copy(q, offset, row_of(offset)).wait_recv()
     own_fin.wait()
     for part in range(2):
         for t in range(tiles):
             out_ref[part, :, t * SIDE:(t + 1) * SIDE] = fin_in[t // 8, part, :, t % 8, :]
 
-    each_row_peer(lambda q: fin_copy(q, my_r).wait_send())
+    for q, offset in enumerate(ROW_OFFSETS[1:]):
+        fin_copy(q, offset, my_r).wait_send()
 
 
 def long_tables(total_rows):
@@ -797,7 +863,7 @@
     lines = pltpu.VMEM((local_rows, 2, groups) + TILE, f32)
     final = pltpu.VMEM((rows_count, 2, in_rows) + TILE, f32)
     return pl.pallas_call(
-        functools.partial(lens_kernel, rows_count, fields_count, local_rows),
+        lens_kernel,
         out_shape=jax.ShapeDtypeStruct((2,) + sky_maps.shape[1:], f32),
         in_specs=[pl.BlockSpec(memory_space=pltpu.SMEM)]
         + [pl.BlockSpec(memory_space=pl.ANY)] * 4
@@ -808,6 +874,7 @@
             pltpu.VMEM((6, local_rows, NC), f32),
             pltpu.VMEM((6, local_rows, SIDE, SIDE), f32),
             slab, slab,
+            pltpu.VMEM((3, 2, in_rows) + TILE, f32),
             pltpu.VMEM((3, local_rows, groups, 2) + TILE, f32),
             pltpu.VMEM((3, local_rows, 2, groups) + TILE, f32),
             pltpu.VMEM((6, local_rows, SIDE, SIDE), f32),
@@ -816,9 +883,9 @@
             pltpu.VMEM((5, 2, total_rows) + TILE, f32),
             pltpu.VMEM((2, total_rows) + TILE, f32),
             chunk, lines, lines, chunk, final, final,
-            dma((2, 3, rows_count)), dma((2, 3, local_rows, groups - 1)),
+            dma((2, 3, rows_count)), dma((2, 3)), dma((3, 2)), dma((2, 3, local_rows, groups - 1)), dma((2, 6)),
             dma((2, local_rows, len(LEG_GROUPS), groups - 1)),
-            dma((2, local_rows, groups - 1)), dma((2, local_rows, groups - 1)),
+            dma((2, local_rows, groups - 1)), dma((2, local_rows, groups)),
             dma((2, rows_count)), dma((4 + (5 + len(LEG_GROUPS)) * local_rows,)),
             dma((4,)),
         ],
@@ -843,10 +910,10 @@
     def choose(sky_maps, *rest):
         fits = (
             NC == SIDE * SIDE
-            and fields_count % 2 == 0
+            and (mesh.shape["sims"], rows_count, fields_count) == (2, 4, 4)
             and NC // groups == TILE[0] * TILE[1]
-            and sky_maps.shape[1] % 8 == 0
-            and sky_maps.shape[1] * rows_count in (16, 32, 64)
+            and sky_maps.shape[0] == 3
+            and sky_maps.shape[1] * rows_count == 32
         )
         if fits:
             return fused_body(rows_count, fields_count, sky_maps, *rest)

time: 84.4 us -> 76.5 us (0.906); the launches traced: 83.4 us -> 76.3 us
  Pallas kernels: 81.7 us -> 74.7 us
    pallas_call x1, Pallas kernels: 81.7 us -> 74.7 us  [fused_body(): pl.pallas_call(lens_kernel, out_shape=jax.ShapeDtypeStruct((2,) + sky_map...]
where the time goes in v1:
time: 76.5 us; the launch traced here: 76.3 us
  Pallas kernels  74.7 us (98%)
  local copies, waits for them, and re-layouts  1.67 us (2%)
    pallas_call x1, Pallas kernels, fused_body(): pl.pallas_call(lens_kernel, out_shape=jax.ShapeDtypeStruct((2,) + sky_map...  74.7 us
    unnamed x1, local copies, waits for them, and re-layouts  1.67 us

profile of v1, /device:TPU:3, one launch (start us, length us, event | category | flops | bytes accessed | tf_op | source)
XLA Modules:
  0.0 76.3 jit_solution(13316355381694236617)
XLA Ops:
  0.0 74.7 %lens.1 = f32[2,8,4096]{2,1,0:T(8,128)} custom-call(s32[6]{0:T(128)} %cuts_ref.1, f32[3,8,4096]{2,1,0:T(8,128)} %sky_hbm.1, f32[3,2,16384]{2,1,0:T(2,128)} %filters_hbm.1, f32[2,2,16384]{2,1,0:T(2,128)} %wiener_hbm.1, f32[2,16384]{1,0:T(2,128)} %response_hbm.1, bf16[2,2,256,256]{3,2,1,0:T(8,128)(2,1)} %constant.4.clone.table_ref, ...), custom_call_target="tpu_custom_call" | custom-call | tf_op jit(solution)/shard_map/lens/pallas_call | solution.py:865
  74.7 1.7 %copy.9 = f32[2,8,4096]{2,1,0:T(8,128)} copy(f32[2,8,4096]{2,1,0:T(8,128)} %lens.1) | data formatting | bytes 524288

commit v2 on v1

--- a/solution.py
+++ b/solution.py
@@ -264,6 +264,7 @@
 SIDE = 128
 TILE = (8, 128)
 LEG_GROUPS = ((0, 2), (2, 2), (4, 1))
+WEIGHT_GROUPS = ((0, 3), (1, 4), (2,), (5,))
 MESH = pl.DeviceIdType.MESH
 
 
@@ -341,14 +342,14 @@
     ((1, 1, 1), (1, 0, 0), (0, 1, 0), (0, 0, 1), (1, 1, 0), (0, 1, 1), (1, 0, 1), (0, 0, 0))
 ]
 PEERS = [offset for offset in OFFSETS if any(offset)]
-WEIGHT_ORDER = (0, 3, 1, 2, 4, 5)
+WEIGHT_ORDER = (0, 3, 1, 4, 2, 5)
 
 
 def lens_kernel(
-    cuts_ref, sky_hbm, filters_hbm, wiener_hbm, response_hbm, table_ref, twiddle_ref, out_ref,
-    sky_ref, raw, weight_ref, slab_out, slab_in, relay_buf, spec_out, spec_in, weights, legs_out, legs_in,
+    cuts_ref, sky_hbm, filters_hbm, wiener_hbm, response_hbm, table_hbm, twiddle_hbm, out_ref,
+    table_ref, twiddle_ref, sky_ref, raw, weight_ref, slab_out, slab_in, relay_buf, spec_out, spec_in, weights, legs_out, legs_in,
     maps, current, cur_out, cur_in, est_out, est_in, fin_out, fin_in,
-    slab_sem, relay_sem, forward_sem, spec_sem, weight_sem, legs_sem, cur_sem, est_sem, fin_sem, self_sem, load_sem,
+    slab_sem, relay_sem, spec_sem, weight_sem, legs_sem, cur_sem, est_sem, fin_sem, send_sem, load_sem,
 ):
     rows_count, fields_count, local_rows = 4, 4, 2
     groups = rows_count * fields_count
@@ -371,9 +372,6 @@
     def peer_block(offset):
         return (2 * x_at[offset[0]] + l_at[offset[2]]) * rows_count + row_of(offset)
 
-    def home_source(offset):
-        return row_of(offset) * fields_count + 2 * h_at[offset[0]] + l_at[offset[2]]
-
     def remote(src, dst, sems, x, r, z):
         return pltpu.make_async_remote_copy(
             src_ref=src, dst_ref=dst, send_sem=sems[0], recv_sem=sems[1],
@@ -387,20 +385,25 @@
         return remote(src, dst, sems, my_h, row_of(offset), 2 * x_at[offset[0]] + l_at[offset[2]])
 
     def each_peer(body):
-        for q, offset in enumerate(PEERS):
-            body(q, offset)
-
-    loads = [
-        pltpu.make_async_copy(src, dst, load_sem.at[n])
-        for n, (src, dst) in enumerate((
-            (sky_hbm, sky_ref),
-            (filters_hbm, raw.at[0:3]),
-            (wiener_hbm, raw.at[3:5]),
-            (response_hbm, raw.at[5]),
-        ))
-    ]
-    for load in loads:
-        load.start()
+        for offset in PEERS:
+            body(offset)
+
+    def wait_all(ref, sem):
+        pltpu.make_async_copy(ref, ref, sem).wait()
+
+    for src, dst, n in (
+        (sky_hbm, sky_ref, 0),
+        (filters_hbm, raw.at[0:3], 1),
+        (wiener_hbm, raw.at[3:5], 1),
+        (response_hbm, raw.at[5], 1),
+        (table_hbm, table_ref, 2),
+        (twiddle_hbm, twiddle_ref, 3),
+    ):
+        pltpu.make_async_copy(src, dst, load_sem.at[n]).start()
+
+    (
+        slab_left, relay_left, forward_left, spec_left, weight_left, legs_left, cur_left, est_left, fin_left,
+    ) = (send_sem.at[n] for n in range(9))
 
     barrier = pltpu.get_barrier_semaphore()
     for h in BITS:
@@ -410,7 +413,7 @@
                     barrier, inc=1, device_id_type=MESH,
                     device_id={"sims": x_at[c], "rows": 2 * y_at[a1] + c_at[a0], "fields": 2 * h_at[h] + l_at[e]},
                 )
-    loads[0].wait()
+    wait_all(sky_ref, load_sem.at[0])
     tiles = sky_ref.shape[2] // SIDE
     for field in range(3):
         for t in range(tiles):
@@ -419,27 +422,27 @@
 
     ROW_OFFSETS = [(0, a1, 0, a0) for a1 in BITS for a0 in BITS]
 
-    def slab_copy(field, offset, source_row):
+    def slab_copy(field, offset):
         r = row_of(offset)
         return send_home(
-            offset, slab_out.at[r, field], slab_in.at[source_row, field],
-            (slab_sem.at[0, field, 2 * offset[1] + offset[3]], slab_sem.at[1, field, 2 * offset[1] + offset[3]]),
+            offset, slab_out.at[r, field], slab_in.at[my_r, field],
+            (slab_left, slab_sem.at[field]),
         )
 
     def own_slab(field):
-        return pltpu.make_async_copy(slab_out.at[my_r, field], slab_in.at[my_r, field], self_sem.at[field])
+        return pltpu.make_async_copy(slab_out.at[my_r, field], slab_in.at[my_r, field], slab_sem.at[field])
 
     def relay_copy(field):
         return remote(
             slab_out.at[pl.ds(2 * y_at[1], 2), field], relay_buf.at[field],
-            (relay_sem.at[0, field], relay_sem.at[1, field]), x_at[1], my_r, my_z,
+            (relay_left, relay_sem.at[field]), x_at[1], my_r, my_z,
         )
 
     def forward_copy(field, core):
         a0 = core
         return remote(
             relay_buf.at[field, c_at[a0]], slab_in.at[my_r, field],
-            (forward_sem.at[field, a0], slab_sem.at[1, field, 2 + a0]),
+            (forward_left, slab_sem.at[field]),
             my_x, 2 * y_at[1] + c_at[a0], 2 * h_at[1] + my_l,
         )
 
@@ -448,14 +451,14 @@
         for field in range(3):
             own_slab(field).start()
             for offset in ROW_OFFSETS[1:]:
-                slab_copy(field, offset, my_r).start()
+                slab_copy(field, offset).start()
 
     @pl.when(jnp.logical_not(stays))
     def _():
         for field in range(3):
             relay_copy(field).start()
             for offset in ROW_OFFSETS[:2]:
-                slab_copy(field, offset, my_r).start()
+                slab_copy(field, offset).start()
 
     low_index = lax.broadcasted_iota(jnp.int32, (SIDE, SIDE), 0)
     high_index = lax.broadcasted_iota(jnp.int32, (SIDE, SIDE), 1)
@@ -466,42 +469,74 @@
         row_id = in_rows * my_r + 4 * (my_h + row - 2 * my_h * row) + 2 * my_l + my_x
         return jnp.where(row_id < total_rows // 2, row_id, row_id - total_rows)
 
+    wait_all(raw, load_sem.at[1])
+
+    def spread(n, carry):
+        for j in range(8):
+            start = pl.multiple_of((n * 8 + j) * SIDE, SIDE)
+            weight_ref[:, :, n * 8 + j, :] = raw[:, :, pl.ds(start, SIDE)]
+        return carry
+
+    lax.fori_loop(0, SIDE // 8, spread, 0)
+    scaled_home = row_ratio * row_frequency(0)
+    radius_home = freq_cols * freq_cols + scaled_home * scaled_home
+
+    def mask(n):
+        low, high = cuts_ref[2 * n], cuts_ref[2 * n + 1]
+        inside = (radius_home >= low * low) & (radius_home <= high * high)
+        return inside.astype(jnp.float32)
+
+    def weight_copy(n):
+        group = [n in members for members in WEIGHT_GROUPS].index(True)
+        return remote(
+            weights.at[n, 0], weights.at[n, 1], (weight_left, weight_sem.at[group]),
+            my_x, my_r, 2 * h_at[1] + my_l,
+        )
+
+    pol = mask(1)
+    weights[0, 0] = mask(0) * weight_ref[0, my_x].T
+    weights[1, 0] = pol * weight_ref[1, my_x].T
+    weights[2, 0] = pol * weight_ref[2, my_x].T
+    weights[3, 0] = weight_ref[3, my_x].T
+    weights[4, 0] = weight_ref[4, my_x].T
+    weights[5, 0] = mask(2) * weight_ref[5, my_x].T
+    weight_copy(WEIGHT_ORDER[0]).start()
+
+    @pl.when(jnp.logical_not(stays))
+    def _():
+        for n in WEIGHT_ORDER[1:]:
+            weight_copy(n).start()
+
     def owner(k):
         return k // 8 * fields_count + 2 * (k % 2) + k // 2 % 2
 
     def local_row(k, half):
         return 1 - half if k // 4 % 2 else half
 
-    def spec_copy(field, row, q, offset, block):
+    def spec_copy(field, row, offset):
         return send(
-            offset, spec_out.at[field, row, peer_of(offset)], spec_in.at[field, row, :, block],
-            (spec_sem.at[0, field, row, q], spec_sem.at[1, field, row, q]),
+            offset, spec_out.at[field, row, peer_of(offset)], spec_in.at[field, row, :, my_block],
+            (spec_left, spec_sem.at[row]),
         )
 
     def own_spec(field, row):
         return pltpu.make_async_copy(
             spec_out.at[field, row, me], spec_in.at[field, row, :, my_block],
-            self_sem.at[3 + field * local_rows + row],
+            spec_sem.at[row],
         )
 
     def spec_start(field, row):
-        each_peer(lambda q, offset: spec_copy(field, row, q, offset, my_block).start())
+        each_peer(lambda offset: spec_copy(field, row, offset).start())
         own_spec(field, row).start()
 
     def row_step(field, carry):
         @pl.when(stays)
         def _():
-            relay_copy(field).wait_recv()
+            wait_all(relay_buf.at[field], relay_sem.at[field])
             for core in BITS:
                 forward_copy(field, core).start()
-            own_slab(field).wait()
-
-        @pl.when(jnp.logical_not(stays))
-        def _():
-            slab_copy(field, ROW_OFFSETS[0], my_r).wait_recv()
-
-        for offset in ROW_OFFSETS[1:]:
-            slab_copy(field, offset, row_of(offset)).wait_recv()
+
+        wait_all(slab_in.at[:, field], slab_sem.at[field])
         values = [
             (slab_in[y // in_rows, field, y % in_rows], None) for y in range(total_rows)
         ]
@@ -515,53 +550,16 @@
 
     lax.fori_loop(0, 3, row_step, 0)
 
+    @pl.when(stays)
+    def _():
+        for n in WEIGHT_ORDER[1:]:
+            weight_copy(n).start()
+
     def later_rows(field, carry):
         spec_start(field, 1)
         return carry
 
     lax.fori_loop(0, 3, later_rows, 0)
-
-    for load in loads[1:]:
-        load.wait()
-
-    def spread(n, carry):
-        for j in range(8):
-            start = pl.multiple_of((n * 8 + j) * SIDE, SIDE)
-            weight_ref[:, :, n * 8 + j, :] = raw[:, :, pl.ds(start, SIDE)]
-        return carry
-
-    lax.fori_loop(0, SIDE // 8, spread, 0)
-    scaled_home = row_ratio * row_frequency(0)
-    radius_home = freq_cols * freq_cols + scaled_home * scaled_home
-
-    def mask(n):
-        low, high = cuts_ref[2 * n], cuts_ref[2 * n + 1]
-        inside = (radius_home >= low * low) & (radius_home <= high * high)
-        return inside.astype(jnp.float32)
-
-    def weight_copy(n):
-        return remote(
-            weights.at[n, 0], weights.at[n, 1], (weight_sem.at[0, n], weight_sem.at[1, n]),
-            my_x, my_r, 2 * h_at[1] + my_l,
-        )
-
-    pol = mask(1)
-    weights[0, 0] = mask(0) * weight_ref[0, my_x].T
-    weights[1, 0] = pol * weight_ref[1, my_x].T
-    weights[2, 0] = pol * weight_ref[2, my_x].T
-    weights[3, 0] = weight_ref[3, my_x].T
-    weights[4, 0] = weight_ref[4, my_x].T
-    weights[5, 0] = mask(2) * weight_ref[5, my_x].T
-    for n in WEIGHT_ORDER:
-        weight_copy(n).start()
-
-    def spec_wait(row):
-        def step(field, carry):
-            each_peer(lambda q, offset: spec_copy(field, row, q, offset, peer_block(offset)).wait_recv())
-            own_spec(field, row).wait()
-            return carry
-
-        lax.fori_loop(0, 3, step, 0)
 
     cos_f, sin_f, cos_b, sin_b = 0, 1, 2, 3
 
@@ -595,14 +593,12 @@
             for n in range(len(pairs))
         ]
 
-    leg_self = 3 + 3 * local_rows
-
-    def legs_copy(row, g, q, offset, source):
+    def legs_copy(row, g, offset):
         first, count = LEG_GROUPS[g]
         return send(
             offset, legs_out.at[row, first:first + count, :, peer_block(offset)],
-            legs_in.at[row, source, first:first + count],
-            (legs_sem.at[0, row, g, q], legs_sem.at[1, row, g, q]),
+            legs_in.at[row, me, first:first + count],
+            (legs_left, legs_sem.at[g]),
         )
 
     def own_legs(row, g):
@@ -610,8 +606,12 @@
         return pltpu.make_async_copy(
             legs_out.at[row, first:first + count, :, my_block],
             legs_in.at[row, me, first:first + count],
-            self_sem.at[leg_self + row * len(LEG_GROUPS) + g],
-        )
+            legs_sem.at[g],
+        )
+
+    def wait_weights(group):
+        members = WEIGHT_GROUPS[group]
+        wait_all(weights.at[0:len(members), 1], weight_sem.at[group])
 
     def slopes(row):
         along_x = (2 * freq_cols).astype(jnp.float32) / NC
@@ -619,13 +619,7 @@
         return along_x, along_y
 
     def leg_step(row, carry):
-        spec_wait(row)
-
-        @pl.when(row == 1)
-        def _():
-            for n in WEIGHT_ORDER[:5]:
-                weight_copy(n).wait_recv()
-
+        wait_all(spec_in.at[:, row], spec_sem.at[row])
         temp, stokes_q, stokes_u = long_forward(
             [spec_in[field, row].reshape(2 * SIDE, SIDE) for field in range(3)]
         )
@@ -637,33 +631,38 @@
         along_x, along_y = slopes(row)
         raising, lowering = (-along_y, along_x), (along_y, along_x)
         rot = (cos2, sin2)
-        w_t, w_e, w_b = weights[0, row], weights[1, row], weights[2, row]
-        w_gt, w_ge = weights[3, row], weights[4, row]
-        t_bar = (w_t * temp[0], w_t * temp[1])
-        e_bar = tuple(-w_e * (cos2 * a + sin2 * b) for a, b in zip(stokes_q, stokes_u))
-        b_bar = tuple(w_b * (sin2 * a - cos2 * b) for a, b in zip(stokes_q, stokes_u))
-        g = complex_mul((w_gt * t_bar[0], w_gt * t_bar[1]), raising)
-        p = complex_mul((b_bar[1] - e_bar[0], -(e_bar[1] + b_bar[0])), rot)
-        w = complex_mul((-w_ge * e_bar[0], -w_ge * e_bar[1]), rot)
-        h3 = complex_mul(w, raising)
-        h1 = complex_mul(w, lowering)
-        legs = (t_bar, g, p, h3, h1)
-        for n, (first, count) in enumerate(LEG_GROUPS):
-            for k, leg_map in enumerate(long_inverse(legs[first:first + count])):
-                legs_out[row, first + k] = leg_map
-            each_peer(lambda q, offset: legs_copy(row, n, q, offset, me).start())
+
+        def temp_legs():
+            t_bar = (weights[0, row] * temp[0], weights[0, row] * temp[1])
+            return t_bar, complex_mul((weights[3, row] * t_bar[0], weights[3, row] * t_bar[1]), raising)
+
+        def e_modes():
+            return tuple(-weights[1, row] * (cos2 * a + sin2 * b) for a, b in zip(stokes_q, stokes_u))
+
+        def spin_legs():
+            e_bar = e_modes()
+            w = complex_mul((-weights[4, row] * e_bar[0], -weights[4, row] * e_bar[1]), rot)
+            return complex_mul(w, raising), complex_mul(w, lowering)
+
+        def pol_leg():
+            e_bar = e_modes()
+            b_bar = tuple(weights[2, row] * (sin2 * a - cos2 * b) for a, b in zip(stokes_q, stokes_u))
+            return (complex_mul((b_bar[1] - e_bar[0], -(e_bar[1] + b_bar[0])), rot),)
+
+        for n, make in enumerate((temp_legs, spin_legs, pol_leg)):
+            @pl.when(row == 1)
+            def _():
+                wait_weights(n)
+
+            for k, leg_map in enumerate(long_inverse(make())):
+                legs_out[row, LEG_GROUPS[n][0] + k] = leg_map
+            each_peer(lambda offset: legs_copy(row, n, offset).start())
             own_legs(row, n).start()
         return carry
 
+    wait_all(table_ref, load_sem.at[2])
+    wait_all(twiddle_ref, load_sem.at[3])
     lax.fori_loop(0, local_rows, leg_step, 0)
-
-    def leg_wait(g):
-        def step(row, carry):
-            each_peer(lambda q, offset: legs_copy(row, g, q, offset, peer_of(offset)).wait_recv())
-            own_legs(row, g).wait()
-            return carry
-
-        lax.fori_loop(0, local_rows, step, 0)
 
     def map_step(n, carry):
         values = [
@@ -676,11 +675,11 @@
         return carry
 
     for g, (first, count) in enumerate(LEG_GROUPS):
-        leg_wait(g)
+        wait_all(legs_in.at[:, :, first:first + count], legs_sem.at[g])
         lax.fori_loop(first, first + count, map_step, 0)
 
     def product_step(y, carry):
-        a, g, p, h3, h1 = [(maps[n, 0, y], maps[n, 1, y]) for n in range(5)]
+        a, g, h3, h1, p = [(maps[n, 0, y], maps[n, 1, y]) for n in range(5)]
         ag, ph, hp = complex_mul(a, g), conj_mul(p, h3), conj_mul(h1, p)
         current[0, y] = ag[0] + 0.5 * (ph[0] + hp[0])
         current[1, y] = ag[1] + 0.5 * (ph[1] + hp[1])
@@ -692,54 +691,51 @@
     for k, (real, imag) in enumerate(short_transform(values, -1)):
         cur_out[local_row(k, my_h), owner(k), 0] = real
         cur_out[local_row(k, my_h), owner(k), 1] = imag
-    cur_self = leg_self + len(LEG_GROUPS) * local_rows
-    est_self = cur_self + local_rows
-
-    def cur_copy(row, q, offset, block):
+
+    def cur_copy(row, offset):
         return send(
-            offset, cur_out.at[row, peer_of(offset)], cur_in.at[row, :, block],
-            (cur_sem.at[0, row, q], cur_sem.at[1, row, q]),
+            offset, cur_out.at[row, peer_of(offset)], cur_in.at[row, :, my_block],
+            (cur_left, cur_sem.at[row]),
         )
 
     def own_cur(row):
         return pltpu.make_async_copy(
-            cur_out.at[row, me], cur_in.at[row, :, my_block], self_sem.at[cur_self + row]
+            cur_out.at[row, me], cur_in.at[row, :, my_block], cur_sem.at[row]
         )
 
     def cur_start(row, carry):
-        each_peer(lambda q, offset: cur_copy(row, q, offset, my_block).start())
+        each_peer(lambda offset: cur_copy(row, offset).start())
         own_cur(row).start()
         return carry
 
     lax.fori_loop(0, local_rows, cur_start, 0)
 
-    def est_copy(row, q, offset, source):
+    def est_copy(row, offset):
         return send_home(
-            offset, est_out.at[row, :, peer_block(offset)], est_in.at[row, source],
-            (est_sem.at[0, row, q], est_sem.at[1, row, q]),
+            offset, est_out.at[row, :, peer_block(offset)], est_in.at[row, me],
+            (est_left, est_sem.at[0]),
         )
 
     ORIGIN = (0, 0, 0, 0)
 
     def own_est(row):
         return pltpu.make_async_copy(
-            est_out.at[row, :, my_block], est_in.at[row, me], self_sem.at[est_self + row]
+            est_out.at[row, :, my_block], est_in.at[row, me], est_sem.at[0]
         )
 
     def estimate_step(row, carry):
-        each_peer(lambda q, offset: cur_copy(row, q, offset, peer_block(offset)).wait_recv())
-        own_cur(row).wait()
+        wait_all(cur_in.at[row], cur_sem.at[row])
 
         @pl.when(row == 1)
         def _():
-            weight_copy(5).wait_recv()
+            wait_weights(3)
 
         (modes,) = long_forward([cur_in[row].reshape(2 * SIDE, SIDE)])
         along_x, along_y = slopes(row)
         w = weights[5, row]
         estimate = complex_mul((w * modes[0], w * modes[1]), (along_y, along_x))
         (est_out[row],) = long_inverse([estimate])
-        each_peer(lambda q, offset: est_copy(row, q, offset, me).start())
+        each_peer(lambda offset: est_copy(row, offset).start())
 
         @pl.when(stays)
         def _():
@@ -747,27 +743,13 @@
 
         @pl.when(jnp.logical_not(stays))
         def _():
-            est_copy(row, groups - 1, ORIGIN, me).start()
+            est_copy(row, ORIGIN).start()
 
         return carry
 
     lax.fori_loop(0, local_rows, estimate_step, 0)
 
-    def est_wait(row, carry):
-        each_peer(lambda q, offset: est_copy(row, q, offset, home_source(offset)).wait_recv())
-
-        @pl.when(stays)
-        def _():
-            own_est(row).wait()
-
-        @pl.when(jnp.logical_not(stays))
-        def _():
-            est_copy(row, groups - 1, ORIGIN, home_source(ORIGIN)).wait_recv()
-
-        return carry
-
-    lax.fori_loop(0, local_rows, est_wait, 0)
-
+    wait_all(est_in, est_sem.at[0])
     values = [
         (est_in[local_row(k, my_x), owner(k), 0], est_in[local_row(k, my_x), owner(k), 1])
         for k in range(total_rows)
@@ -776,61 +758,43 @@
         fin_out[y // in_rows, 0, y % in_rows] = real
         fin_out[y // in_rows, 1, y % in_rows] = imag
 
-    def fin_copy(q, offset, source_row):
+    def fin_copy(offset):
         r = row_of(offset)
         return remote(
-            fin_out.at[r], fin_in.at[source_row], (fin_sem.at[0, q], fin_sem.at[1, q]), my_x, r, my_z
-        )
-
-    for q, offset in enumerate(ROW_OFFSETS[1:]):
-        fin_copy(q, offset, my_r).start()
+            fin_out.at[r], fin_in.at[my_r], (fin_left, fin_sem.at[0]), my_x, r, my_z
+        )
+
+    for offset in ROW_OFFSETS[1:]:
+        fin_copy(offset).start()
     own_fin = pltpu.make_async_copy(
-        fin_out.at[my_r], fin_in.at[my_r], self_sem.at[est_self + local_rows]
+        fin_out.at[my_r], fin_in.at[my_r], fin_sem.at[0]
     )
     own_fin.start()
+
+    others = groups - 1
 
     @pl.when(stays)
     def _():
-        for field in range(3):
-            for offset in ROW_OFFSETS[1:]:
-                slab_copy(field, offset, my_r).wait_send()
-            for core in BITS:
-                forward_copy(field, core).wait_send()
+        wait_all(slab_out.at[0:3], slab_left)
+        wait_all(relay_buf, forward_left)
+        wait_all(est_out.at[:, :, 0:others], est_left)
 
     @pl.when(jnp.logical_not(stays))
     def _():
-        for field in range(3):
-            relay_copy(field).wait_send()
-            for offset in ROW_OFFSETS[:2]:
-                slab_copy(field, offset, my_r).wait_send()
-        for row in range(local_rows):
-            est_copy(row, groups - 1, ORIGIN, me).wait_send()
-
-    for n in WEIGHT_ORDER:
-        weight_copy(n).wait_send()
-
-    def sends_left(row, carry):
-        def spec_left(field, inner):
-            each_peer(lambda q, offset: spec_copy(field, row, q, offset, my_block).wait_send())
-            return inner
-
-        lax.fori_loop(0, 3, spec_left, 0)
-        for g in range(len(LEG_GROUPS)):
-            each_peer(lambda q, offset: legs_copy(row, g, q, offset, me).wait_send())
-        each_peer(lambda q, offset: cur_copy(row, q, offset, my_block).wait_send())
-        each_peer(lambda q, offset: est_copy(row, q, offset, me).wait_send())
-        return carry
-
-    lax.fori_loop(0, local_rows, sends_left, 0)
-    for q, offset in enumerate(ROW_OFFSETS[1:]):
-        fin_copy(q, offset, row_of(offset)).wait_recv()
-    own_fin.wait()
+        wait_all(slab_out.at[0:2], slab_left)
+        wait_all(relay_buf, relay_left)
+        wait_all(est_out, est_left)
+
+    wait_all(weights.at[:, 0], weight_left)
+    wait_all(spec_out.at[:, :, 0:others], spec_left)
+    wait_all(legs_out.at[:, :, :, 0:others], legs_left)
+    wait_all(cur_out.at[:, 0:others], cur_left)
+    wait_all(fin_in, fin_sem.at[0])
     for part in range(2):
         for t in range(tiles):
             out_ref[part, :, t * SIDE:(t + 1) * SIDE] = fin_in[t // 8, part, :, t % 8, :]
 
-    for q, offset in enumerate(ROW_OFFSETS[1:]):
-        fin_copy(q, offset, my_r).wait_send()
+    wait_all(fin_out.at[0:3], fin_left)
 
 
 def long_tables(total_rows):
@@ -865,11 +829,10 @@
     return pl.pallas_call(
         lens_kernel,
         out_shape=jax.ShapeDtypeStruct((2,) + sky_maps.shape[1:], f32),
-        in_specs=[pl.BlockSpec(memory_space=pltpu.SMEM)]
-        + [pl.BlockSpec(memory_space=pl.ANY)] * 4
-        + [vmem] * 2,
+        in_specs=[pl.BlockSpec(memory_space=pltpu.SMEM)] + [pl.BlockSpec(memory_space=pl.ANY)] * 6,
         out_specs=vmem,
         scratch_shapes=[
+            pltpu.VMEM(table.shape, table.dtype), pltpu.VMEM(twiddle.shape, f32),
             pltpu.VMEM(sky_maps.shape, f32),
             pltpu.VMEM((6, local_rows, NC), f32),
             pltpu.VMEM((6, local_rows, SIDE, SIDE), f32),
@@ -883,11 +846,8 @@
             pltpu.VMEM((5, 2, total_rows) + TILE, f32),
             pltpu.VMEM((2, total_rows) + TILE, f32),
             chunk, lines, lines, chunk, final, final,
-            dma((2, 3, rows_count)), dma((2, 3)), dma((3, 2)), dma((2, 3, local_rows, groups - 1)), dma((2, 6)),
-            dma((2, local_rows, len(LEG_GROUPS), groups - 1)),
-            dma((2, local_rows, groups - 1)), dma((2, local_rows, groups)),
-            dma((2, rows_count)), dma((4 + (5 + len(LEG_GROUPS)) * local_rows,)),
-            dma((4,)),
+            dma((3,)), dma((3,)), dma((local_rows,)), dma((len(WEIGHT_GROUPS),)), dma((len(LEG_GROUPS),)),
+            dma((local_rows,)), dma((1,)), dma((1,)), dma((9,)), dma((4,)),
         ],
         compiler_params=pltpu.CompilerParams(
             collective_id=0, has_side_effects=True, vmem_limit_bytes=60 * 1024 * 1024

time: 76.5 us -> 70.4 us (0.920)
  Pallas kernels: 74.7 us -> 68.6 us
    pallas_call x1, Pallas kernels: 74.7 us -> 68.6 us  [fused_body(): pl.pallas_call(lens_kernel, out_shape=jax.ShapeDtypeStruct((2,) + sky_map...]
where the time goes in v2:
time: 70.4 us; the launch traced here: 70.2 us
  Pallas kernels  68.6 us (97%)
  local copies, waits for them, and re-layouts  1.67 us (2%)
    pallas_call x1, Pallas kernels, fused_body(): pl.pallas_call(lens_kernel, out_shape=jax.ShapeDtypeStruct((2,) + sky_map...  68.6 us
    unnamed x1, local copies, waits for them, and re-layouts  1.67 us

profile of v2, /device:TPU:3, one launch (start us, length us, event | category | flops | bytes accessed | tf_op | source)
XLA Modules:
  0.0 70.2 jit_solution(18294631922923099518)
XLA Ops:
  0.0 68.6 %lens.1 = f32[2,8,4096]{2,1,0:T(8,128)} custom-call(s32[6]{0:T(128)} %cuts_ref.1, f32[3,8,4096]{2,1,0:T(8,128)} %sky_hbm.1, f32[3,2,16384]{2,1,0:T(2,128)} %filters_hbm.1, f32[2,2,16384]{2,1,0:T(2,128)} %wiener_hbm.1, f32[2,16384]{1,0:T(2,128)} %response_hbm.1, bf16[2,2,256,256]{3,2,1,0:T(8,128)(2,1)} %constant.4.clone.table_hbm, ...), custom_call_target="tpu_custom_call" | custom-call | tf_op jit(solution)/shard_map/lens/pallas_call | solution.py:829
  68.6 1.7 %copy.9 = f32[2,8,4096]{2,1,0:T(8,128)} copy(f32[2,8,4096]{2,1,0:T(8,128)} %lens.1) | data formatting | bytes 524288

commit v3 on v2

--- a/solution.py
+++ b/solution.py
@@ -347,7 +347,7 @@
 
 def lens_kernel(
     cuts_ref, sky_hbm, filters_hbm, wiener_hbm, response_hbm, table_hbm, twiddle_hbm, out_ref,
-    table_ref, twiddle_ref, sky_ref, raw, weight_ref, slab_out, slab_in, relay_buf, spec_out, spec_in, weights, legs_out, legs_in,
+    table_ref, twiddle_ref, sky_ref, raw, weight_ref, slab_out, slab_in, relay_buf, spec_out, spec_in, weights, modes, legs_out, legs_in,
     maps, current, cur_out, cur_in, est_out, est_in, fin_out, fin_in,
     slab_sem, relay_sem, spec_sem, weight_sem, legs_sem, cur_sem, est_sem, fin_sem, send_sem, load_sem,
 ):
@@ -363,6 +363,16 @@
     my_block = (2 * my_x + my_l) * rows_count + my_r
     stays = my_x == my_h
 
+    half_rows = total_rows // 2
+    corner = my_x + my_l == 0
+    far = jnp.logical_and(corner, my_y == 1)
+    near = jnp.logical_and(corner, my_y == 0)
+    home_row = in_rows * my_r + 4 * my_h + 2 * my_l + my_x
+    first_row = jnp.where(corner, in_rows * my_c + 4 * (my_h + my_y - 2 * my_h * my_y), home_row)
+
+    def signed(row):
+        return jnp.where(row < half_rows, row, row - total_rows)
+
     def row_of(offset):
         return 2 * y_at[offset[1]] + c_at[offset[3]]
 
@@ -403,7 +413,8 @@
 
     (
         slab_left, relay_left, forward_left, spec_left, weight_left, legs_left, cur_left, est_left, fin_left,
-    ) = (send_sem.at[n] for n in range(9))
+        extra_left,
+    ) = (send_sem.at[n] for n in range(10))
 
     barrier = pltpu.get_barrier_semaphore()
     for h in BITS:
@@ -466,8 +477,7 @@
     freq_cols = jnp.where(column_ids < NC // 2, column_ids, column_ids - NC)
 
     def row_frequency(row):
-        row_id = in_rows * my_r + 4 * (my_h + row - 2 * my_h * row) + 2 * my_l + my_x
-        return jnp.where(row_id < total_rows // 2, row_id, row_id - total_rows)
+        return jnp.where(first_row == 0, -half_rows * row, signed(first_row) * (1 - 2 * row))
 
     wait_all(raw, load_sem.at[1])
 
@@ -478,7 +488,7 @@
         return carry
 
     lax.fori_loop(0, SIDE // 8, spread, 0)
-    scaled_home = row_ratio * row_frequency(0)
+    scaled_home = row_ratio * signed(home_row)
     radius_home = freq_cols * freq_cols + scaled_home * scaled_home
 
     def mask(n):
@@ -486,48 +496,70 @@
         inside = (radius_home >= low * low) & (radius_home <= high * high)
         return inside.astype(jnp.float32)
 
+    home_slot = jnp.where(far, 2, 0)
+    slot = jnp.where(near, 0, 1)
+    other_r = jnp.where(near, my_r + 2, jnp.where(far, jnp.where(my_h == 0, my_r, 5 - my_r), 3 - my_r))
+
     def weight_copy(n):
         group = [n in members for members in WEIGHT_GROUPS].index(True)
         return remote(
-            weights.at[n, 0], weights.at[n, 1], (weight_left, weight_sem.at[group]),
-            my_x, my_r, 2 * h_at[1] + my_l,
-        )
+            weights.at[n, home_slot], weights.at[n, slot], (weight_left, weight_sem.at[slot, group]),
+            my_x, other_r, 2 * h_at[1] + jnp.where(my_x == 1, 1 - my_l, my_l),
+        )
+
+    def extra_copy(n):
+        group = [n in members for members in WEIGHT_GROUPS].index(True)
+        return remote(
+            weights.at[n, home_slot], weights.at[n, 1], (extra_left, weight_sem.at[1, group]),
+            my_x, jnp.where(my_h == 0, my_r - 2, 3 - my_r), my_z,
+        )
+
+    def weight_start(n):
+        weight_copy(n).start()
+
+        @pl.when(far)
+        def _():
+            extra_copy(n).start()
 
     pol = mask(1)
-    weights[0, 0] = mask(0) * weight_ref[0, my_x].T
-    weights[1, 0] = pol * weight_ref[1, my_x].T
-    weights[2, 0] = pol * weight_ref[2, my_x].T
-    weights[3, 0] = weight_ref[3, my_x].T
-    weights[4, 0] = weight_ref[4, my_x].T
-    weights[5, 0] = mask(2) * weight_ref[5, my_x].T
-    weight_copy(WEIGHT_ORDER[0]).start()
+    weights[0, home_slot] = mask(0) * weight_ref[0, my_x].T
+    weights[1, home_slot] = pol * weight_ref[1, my_x].T
+    weights[2, home_slot] = pol * weight_ref[2, my_x].T
+    weights[3, home_slot] = weight_ref[3, my_x].T
+    weights[4, home_slot] = weight_ref[4, my_x].T
+    weights[5, home_slot] = mask(2) * weight_ref[5, my_x].T
+    weight_start(WEIGHT_ORDER[0])
 
     @pl.when(jnp.logical_not(stays))
     def _():
-        for n in WEIGHT_ORDER[1:]:
-            weight_copy(n).start()
+        for n in WEIGHT_ORDER[1:5]:
+            weight_start(n)
 
     def owner(k):
         return k // 8 * fields_count + 2 * (k % 2) + k // 2 % 2
 
-    def local_row(k, half):
-        return 1 - half if k // 4 % 2 else half
-
-    def spec_copy(field, row, offset):
+    def place(k, half):
+        if k % 4 == 0:
+            base = k % half_rows if k <= half_rows else total_rows - k
+            upper = half if base % 8 == 0 else 1 - half
+            return int(k >= half_rows), (base // in_rows + 2 * upper) * fields_count
+        away = 1 - half if k // 4 % 2 else half
+        return away, owner(k) + away * (owner(total_rows - k) - owner(k))
+
+    def spec_copy(field, offset):
         return send(
-            offset, spec_out.at[field, row, peer_of(offset)], spec_in.at[field, row, :, my_block],
-            (spec_left, spec_sem.at[row]),
-        )
-
-    def own_spec(field, row):
+            offset, spec_out.at[field, 0, peer_of(offset)], spec_in.at[field, :, my_block],
+            (spec_left, spec_sem.at[field]),
+        )
+
+    def own_spec(field):
         return pltpu.make_async_copy(
-            spec_out.at[field, row, me], spec_in.at[field, row, :, my_block],
-            spec_sem.at[row],
-        )
-
-    def spec_start(field, row):
-        each_peer(lambda offset: spec_copy(field, row, offset).start())
-        own_spec(field, row).start()
+            spec_out.at[field, 0, me], spec_in.at[field, :, my_block], spec_sem.at[field]
+        )
+
+    def spec_start(field):
+        each_peer(lambda offset: spec_copy(field, offset).start())
+        own_spec(field).start()
 
     def row_step(field, carry):
         @pl.when(stays)
@@ -540,26 +572,23 @@
         values = [
             (slab_in[y // in_rows, field, y % in_rows], None) for y in range(total_rows)
         ]
-        for k, (real, imag) in enumerate(short_transform(values, -1)):
-            spec_out[field, local_row(k, my_h), owner(k), 0] = real
-            spec_out[field, local_row(k, my_h), owner(k), 1] = (
-                jnp.zeros_like(real) if imag is None else imag
-            )
-        spec_start(field, 0)
+        lines = short_transform(values, -1)
+        lines[0] = (lines[0][0], lines[half_rows][0])
+        for k, (real, imag) in enumerate(lines):
+            if k % 4 == 0 and k >= half_rows:
+                continue
+            local, device = place(k, my_h)
+            spec_out[field, local, device, 0] = real
+            spec_out[field, local, device, 1] = imag
+        spec_start(field)
         return carry
 
     lax.fori_loop(0, 3, row_step, 0)
 
     @pl.when(stays)
     def _():
-        for n in WEIGHT_ORDER[1:]:
-            weight_copy(n).start()
-
-    def later_rows(field, carry):
-        spec_start(field, 1)
-        return carry
-
-    lax.fori_loop(0, 3, later_rows, 0)
+        for n in WEIGHT_ORDER[1:5]:
+            weight_start(n)
 
     cos_f, sin_f, cos_b, sin_b = 0, 1, 2, 3
 
@@ -609,20 +638,30 @@
             legs_sem.at[g],
         )
 
-    def wait_weights(group):
+    def wait_weights(group, row):
         members = WEIGHT_GROUPS[group]
-        wait_all(weights.at[0:len(members), 1], weight_sem.at[group])
+
+        @pl.when(jnp.logical_or(row == 1, far))
+        def _():
+            wait_all(weights.at[0:len(members), row], weight_sem.at[row, group])
 
     def slopes(row):
         along_x = (2 * freq_cols).astype(jnp.float32) / NC
         along_y = (2 * row_frequency(row)).astype(jnp.float32) / total_rows
         return along_x, along_y
 
+    packed = jnp.where(first_row == 0, 0.5, 0.0)
+
+    def both_rows(field):
+        wait_all(spec_in.at[field], spec_sem.at[field])
+        line = spec_in[field].reshape(2 * SIDE, SIDE)
+        (ar, ai), (br, bi) = long_forward([line, jnp.concatenate([line[:SIDE], -line[SIDE:]], axis=0)])
+        modes[field, 0, 0] = (1.0 - packed) * ar + packed * br
+        modes[field, 0, 1] = (1.0 - packed) * ai + packed * bi
+        modes[field, 1, 0] = (1.0 - 2.0 * packed) * br + packed * (ai - bi)
+        modes[field, 1, 1] = (1.0 - 2.0 * packed) * bi + packed * (br - ar)
+
     def leg_step(row, carry):
-        wait_all(spec_in.at[:, row], spec_sem.at[row])
-        temp, stokes_q, stokes_u = long_forward(
-            [spec_in[field, row].reshape(2 * SIDE, SIDE) for field in range(3)]
-        )
         scaled = row_ratio * row_frequency(row)
         radius_sq = freq_cols * freq_cols + scaled * scaled
         floor = jnp.maximum(radius_sq, 1).astype(jnp.float32)
@@ -633,11 +672,13 @@
         rot = (cos2, sin2)
 
         def temp_legs():
-            t_bar = (weights[0, row] * temp[0], weights[0, row] * temp[1])
+            t_bar = (weights[0, row] * modes[0, row, 0], weights[0, row] * modes[0, row, 1])
             return t_bar, complex_mul((weights[3, row] * t_bar[0], weights[3, row] * t_bar[1]), raising)
 
         def e_modes():
-            return tuple(-weights[1, row] * (cos2 * a + sin2 * b) for a, b in zip(stokes_q, stokes_u))
+            return tuple(
+                -weights[1, row] * (cos2 * modes[1, row, n] + sin2 * modes[2, row, n]) for n in range(2)
+            )
 
         def spin_legs():
             e_bar = e_modes()
@@ -646,14 +687,19 @@
 
         def pol_leg():
             e_bar = e_modes()
-            b_bar = tuple(weights[2, row] * (sin2 * a - cos2 * b) for a, b in zip(stokes_q, stokes_u))
+            b_bar = tuple(
+                weights[2, row] * (sin2 * modes[1, row, n] - cos2 * modes[2, row, n]) for n in range(2)
+            )
             return (complex_mul((b_bar[1] - e_bar[0], -(e_bar[1] + b_bar[0])), rot),)
 
         for n, make in enumerate((temp_legs, spin_legs, pol_leg)):
-            @pl.when(row == 1)
-            def _():
-                wait_weights(n)
-
+            if n == 1:
+                @pl.when(row == 0)
+                def _():
+                    both_rows(1)
+                    both_rows(2)
+
+            wait_weights(n, row)
             for k, leg_map in enumerate(long_inverse(make())):
                 legs_out[row, LEG_GROUPS[n][0] + k] = leg_map
             each_peer(lambda offset: legs_copy(row, n, offset).start())
@@ -662,11 +708,13 @@
 
     wait_all(table_ref, load_sem.at[2])
     wait_all(twiddle_ref, load_sem.at[3])
+    both_rows(0)
     lax.fori_loop(0, local_rows, leg_step, 0)
+    weight_start(5)
 
     def map_step(n, carry):
         values = [
-            (legs_in[local_row(k, my_h), owner(k), n, 0], legs_in[local_row(k, my_h), owner(k), n, 1])
+            (legs_in[place(k, my_h) + (n, 0)], legs_in[place(k, my_h) + (n, 1)])
             for k in range(total_rows)
         ]
         for y, (real, imag) in enumerate(short_transform(values, 1)):
@@ -689,8 +737,8 @@
 
     values = [(current[0, y], current[1, y]) for y in range(total_rows)]
     for k, (real, imag) in enumerate(short_transform(values, -1)):
-        cur_out[local_row(k, my_h), owner(k), 0] = real
-        cur_out[local_row(k, my_h), owner(k), 1] = imag
+        cur_out[place(k, my_h) + (0,)] = real
+        cur_out[place(k, my_h) + (1,)] = imag
 
     def cur_copy(row, offset):
         return send(
@@ -725,10 +773,7 @@
 
     def estimate_step(row, carry):
         wait_all(cur_in.at[row], cur_sem.at[row])
-
-        @pl.when(row == 1)
-        def _():
-            wait_weights(3)
+        wait_weights(3, row)
 
         (modes,) = long_forward([cur_in[row].reshape(2 * SIDE, SIDE)])
         along_x, along_y = slopes(row)
@@ -751,7 +796,7 @@
 
     wait_all(est_in, est_sem.at[0])
     values = [
-        (est_in[local_row(k, my_x), owner(k), 0], est_in[local_row(k, my_x), owner(k), 1])
+        (est_in[place(k, my_x) + (0,)], est_in[place(k, my_x) + (1,)])
         for k in range(total_rows)
     ]
     for y, (real, imag) in enumerate(short_transform(values, 1)):
@@ -785,8 +830,12 @@
         wait_all(relay_buf, relay_left)
         wait_all(est_out, est_left)
 
+    @pl.when(far)
+    def _():
+        wait_all(weights.at[:, 0], extra_left)
+
     wait_all(weights.at[:, 0], weight_left)
-    wait_all(spec_out.at[:, :, 0:others], spec_left)
+    wait_all(spec_out.at[:, 0, 0:others], spec_left)
     wait_all(legs_out.at[:, :, :, 0:others], legs_left)
     wait_all(cur_out.at[:, 0:others], cur_left)
     wait_all(fin_in, fin_sem.at[0])
@@ -839,15 +888,16 @@
             slab, slab,
             pltpu.VMEM((3, 2, in_rows) + TILE, f32),
             pltpu.VMEM((3, local_rows, groups, 2) + TILE, f32),
-            pltpu.VMEM((3, local_rows, 2, groups) + TILE, f32),
-            pltpu.VMEM((6, local_rows, SIDE, SIDE), f32),
+            pltpu.VMEM((3, 2, groups) + TILE, f32),
+            pltpu.VMEM((6, 3, SIDE, SIDE), f32),
+            pltpu.VMEM((3, local_rows, 2, SIDE, SIDE), f32),
             pltpu.VMEM((local_rows, 5, 2, groups) + TILE, f32),
             pltpu.VMEM((local_rows, groups, 5, 2) + TILE, f32),
             pltpu.VMEM((5, 2, total_rows) + TILE, f32),
             pltpu.VMEM((2, total_rows) + TILE, f32),
             chunk, lines, lines, chunk, final, final,
-            dma((3,)), dma((3,)), dma((local_rows,)), dma((len(WEIGHT_GROUPS),)), dma((len(LEG_GROUPS),)),
-            dma((local_rows,)), dma((1,)), dma((1,)), dma((9,)), dma((4,)),
+            dma((3,)), dma((3,)), dma((3,)), dma((local_rows, len(WEIGHT_GROUPS))), dma((len(LEG_GROUPS),)),
+            dma((local_rows,)), dma((1,)), dma((1,)), dma((10,)), dma((4,)),
         ],
         compiler_params=pltpu.CompilerParams(
             collective_id=0, has_side_effects=True, vmem_limit_bytes=60 * 1024 * 1024

time: 70.4 us -> 72.2 us (1.026)
  Pallas kernels: 68.6 us -> 70.3 us
    pallas_call x1, Pallas kernels: 68.6 us -> 70.3 us  [fused_body(): pl.pallas_call(lens_kernel, out_shape=jax.ShapeDtypeStruct((2,) + sky_map...]
where the time goes in v3:
time: 72.2 us; the launch traced here: 72 us
  Pallas kernels  70.3 us (97%)
  local copies, waits for them, and re-layouts  1.67 us (2%)
    pallas_call x1, Pallas kernels, fused_body(): pl.pallas_call(lens_kernel, out_shape=jax.ShapeDtypeStruct((2,) + sky_map...  70.3 us
    unnamed x1, local copies, waits for them, and re-layouts  1.67 us

profile of v3, /device:TPU:3, one launch (start us, length us, event | category | flops | bytes accessed | tf_op | source)
XLA Modules:
  0.0 72.0 jit_solution(13297640414112007912)
XLA Ops:
  0.0 70.3 %lens.1 = f32[2,8,4096]{2,1,0:T(8,128)} custom-call(s32[6]{0:T(128)} %cuts_ref.1, f32[3,8,4096]{2,1,0:T(8,128)} %sky_hbm.1, f32[3,2,16384]{2,1,0:T(2,128)} %filters_hbm.1, f32[2,2,16384]{2,1,0:T(2,128)} %wiener_hbm.1, f32[2,16384]{1,0:T(2,128)} %response_hbm.1, bf16[2,2,256,256]{3,2,1,0:T(8,128)(2,1)} %constant.4.clone.table_hbm, ...), custom_call_target="tpu_custom_call" | custom-call | tf_op jit(solution)/shard_map/lens/pallas_call | solution.py:878
  70.3 1.7 %copy.9 = f32[2,8,4096]{2,1,0:T(8,128)} copy(f32[2,8,4096]{2,1,0:T(8,128)} %lens.1) | data formatting | bytes 524288

commit v4 on v3

--- a/solution.py
+++ b/solution.py
@@ -347,9 +347,9 @@
 
 def lens_kernel(
     cuts_ref, sky_hbm, filters_hbm, wiener_hbm, response_hbm, table_hbm, twiddle_hbm, out_ref,
-    table_ref, twiddle_ref, sky_ref, raw, weight_ref, slab_out, slab_in, relay_buf, spec_out, spec_in, weights, modes, legs_out, legs_in,
+    table_ref, twiddle_ref, sky_ref, raw, weight_ref, slab_out, slab_in, relay_buf, relay_weights, spec_out, spec_in, weights, modes, legs_out, legs_in,
     maps, current, cur_out, cur_in, est_out, est_in, fin_out, fin_in,
-    slab_sem, relay_sem, spec_sem, weight_sem, legs_sem, cur_sem, est_sem, fin_sem, send_sem, load_sem,
+    slab_sem, relay_sem, spec_sem, weight_sem, hand_sem, legs_sem, cur_sem, est_sem, fin_sem, send_sem, load_sem,
 ):
     rows_count, fields_count, local_rows = 4, 4, 2
     groups = rows_count * fields_count
@@ -413,8 +413,8 @@
 
     (
         slab_left, relay_left, forward_left, spec_left, weight_left, legs_left, cur_left, est_left, fin_left,
-        extra_left,
-    ) = (send_sem.at[n] for n in range(10))
+        extra_left, pass_left,
+    ) = (send_sem.at[n] for n in range(11))
 
     barrier = pltpu.get_barrier_semaphore()
     for h in BITS:
@@ -464,12 +464,14 @@
             for offset in ROW_OFFSETS[1:]:
                 slab_copy(field, offset).start()
 
+    def slab_start(field):
+        relay_copy(field).start()
+        for offset in ROW_OFFSETS[:2]:
+            slab_copy(field, offset).start()
+
     @pl.when(jnp.logical_not(stays))
     def _():
-        for field in range(3):
-            relay_copy(field).start()
-            for offset in ROW_OFFSETS[:2]:
-                slab_copy(field, offset).start()
+        slab_start(0)
 
     low_index = lax.broadcasted_iota(jnp.int32, (SIDE, SIDE), 0)
     high_index = lax.broadcasted_iota(jnp.int32, (SIDE, SIDE), 1)
@@ -497,29 +499,59 @@
         return inside.astype(jnp.float32)
 
     home_slot = jnp.where(far, 2, 0)
-    slot = jnp.where(near, 0, 1)
-    other_r = jnp.where(near, my_r + 2, jnp.where(far, jnp.where(my_h == 0, my_r, 5 - my_r), 3 - my_r))
-
-    def weight_copy(n):
-        group = [n in members for members in WEIGHT_GROUPS].index(True)
+    outer = my_l == my_h
+    inner = my_l != my_h
+
+    def group_of(n):
+        return [n in members for members in WEIGHT_GROUPS].index(True)
+
+    def weight_copy(n, source, low, sem):
+        cornered = my_x + low == 0
+        upper, lower = jnp.logical_and(cornered, my_y == 0), jnp.logical_and(cornered, my_y == 1)
+        other_r = jnp.where(upper, my_r + 2, jnp.where(lower, jnp.where(my_h == 0, my_r, 5 - my_r), 3 - my_r))
+        slot = jnp.where(upper, 0, 1)
         return remote(
-            weights.at[n, home_slot], weights.at[n, slot], (weight_left, weight_sem.at[slot, group]),
-            my_x, other_r, 2 * h_at[1] + jnp.where(my_x == 1, 1 - my_l, my_l),
+            source, weights.at[n, slot], (sem, weight_sem.at[slot, group_of(n)]),
+            my_x, other_r, 2 * h_at[1] + jnp.where(my_x == 1, 1 - low, low),
+        )
+
+    def own_weight(n):
+        return weight_copy(n, weights.at[n, home_slot], my_l, weight_left)
+
+    def hand_copy(n):
+        return remote(
+            weights.at[n, home_slot], relay_weights.at[n], (weight_left, hand_sem.at[n]),
+            my_x, my_r, 2 * my_h + l_at[1],
         )
 
     def extra_copy(n):
-        group = [n in members for members in WEIGHT_GROUPS].index(True)
         return remote(
-            weights.at[n, home_slot], weights.at[n, 1], (extra_left, weight_sem.at[1, group]),
+            weights.at[n, home_slot], weights.at[n, 1], (extra_left, weight_sem.at[1, group_of(n)]),
             my_x, jnp.where(my_h == 0, my_r - 2, 3 - my_r), my_z,
         )
 
-    def weight_start(n):
-        weight_copy(n).start()
+    def weight_start(members):
+        @pl.when(outer)
+        def _():
+            for n in members:
+                hand_copy(n).start()
+
+        @pl.when(inner)
+        def _():
+            for n in members:
+                own_weight(n).start()
 
         @pl.when(far)
         def _():
-            extra_copy(n).start()
+            for n in members:
+                extra_copy(n).start()
+
+    def weight_pass_on(members):
+        @pl.when(inner)
+        def _():
+            for n in members:
+                wait_all(relay_weights.at[n], hand_sem.at[n])
+                weight_copy(n, relay_weights.at[n], l_at[1], pass_left).start()
 
     pol = mask(1)
     weights[0, home_slot] = mask(0) * weight_ref[0, my_x].T
@@ -528,12 +560,29 @@
     weights[3, home_slot] = weight_ref[3, my_x].T
     weights[4, home_slot] = weight_ref[4, my_x].T
     weights[5, home_slot] = mask(2) * weight_ref[5, my_x].T
-    weight_start(WEIGHT_ORDER[0])
-
-    @pl.when(jnp.logical_not(stays))
-    def _():
-        for n in WEIGHT_ORDER[1:5]:
-            weight_start(n)
+    @pl.when(jnp.logical_and(inner, jnp.logical_not(stays)))
+    def _():
+        slab_start(1)
+        slab_start(2)
+        for n in WEIGHT_ORDER[:5]:
+            own_weight(n).start()
+
+    @pl.when(jnp.logical_and(outer, jnp.logical_not(stays)))
+    def _():
+        hand_copy(0).start()
+        slab_start(1)
+        hand_copy(3).start()
+        slab_start(2)
+        hand_copy(1).start()
+
+    @pl.when(jnp.logical_and(inner, stays))
+    def _():
+        own_weight(0).start()
+
+    @pl.when(jnp.logical_and(outer, stays))
+    def _():
+        hand_copy(0).start()
+        hand_copy(3).start()
 
     def owner(k):
         return k // 8 * fields_count + 2 * (k % 2) + k // 2 % 2
@@ -561,12 +610,23 @@
         each_peer(lambda offset: spec_copy(field, offset).start())
         own_spec(field).start()
 
-    def row_step(field, carry):
+    def row_step(field):
         @pl.when(stays)
         def _():
             wait_all(relay_buf.at[field], relay_sem.at[field])
             for core in BITS:
                 forward_copy(field, core).start()
+
+        if field == 1:
+            @pl.when(jnp.logical_and(outer, stays))
+            def _():
+                hand_copy(1).start()
+
+        if field == 2:
+            @pl.when(jnp.logical_and(inner, stays))
+            def _():
+                for n in WEIGHT_ORDER[1:5]:
+                    own_weight(n).start()
 
         wait_all(slab_in.at[:, field], slab_sem.at[field])
         values = [
@@ -581,14 +641,21 @@
             spec_out[field, local, device, 0] = real
             spec_out[field, local, device, 1] = imag
         spec_start(field)
-        return carry
-
-    lax.fori_loop(0, 3, row_step, 0)
-
-    @pl.when(stays)
-    def _():
-        for n in WEIGHT_ORDER[1:5]:
-            weight_start(n)
+
+    for field in range(3):
+        row_step(field)
+
+    @pl.when(outer)
+    def _():
+        hand_copy(4).start()
+        hand_copy(2).start()
+
+    @pl.when(far)
+    def _():
+        for n in WEIGHT_ORDER[:5]:
+            extra_copy(n).start()
+
+    weight_pass_on((0, 3, 1))
 
     cos_f, sin_f, cos_b, sin_b = 0, 1, 2, 3
 
@@ -661,7 +728,7 @@
         modes[field, 1, 0] = (1.0 - 2.0 * packed) * br + packed * (ai - bi)
         modes[field, 1, 1] = (1.0 - 2.0 * packed) * bi + packed * (br - ar)
 
-    def leg_step(row, carry):
+    def leg_step(n, row):
         scaled = row_ratio * row_frequency(row)
         radius_sq = freq_cols * freq_cols + scaled * scaled
         floor = jnp.maximum(radius_sq, 1).astype(jnp.float32)
@@ -692,25 +759,41 @@
             )
             return (complex_mul((b_bar[1] - e_bar[0], -(e_bar[1] + b_bar[0])), rot),)
 
-        for n, make in enumerate((temp_legs, spin_legs, pol_leg)):
-            if n == 1:
-                @pl.when(row == 0)
-                def _():
-                    both_rows(1)
-                    both_rows(2)
-
-            wait_weights(n, row)
-            for k, leg_map in enumerate(long_inverse(make())):
-                legs_out[row, LEG_GROUPS[n][0] + k] = leg_map
-            each_peer(lambda offset: legs_copy(row, n, offset).start())
-            own_legs(row, n).start()
-        return carry
+        wait_weights(n, row)
+        for k, leg_map in enumerate(long_inverse((temp_legs, spin_legs, pol_leg)[n]())):
+            legs_out[row, LEG_GROUPS[n][0] + k] = leg_map
+        each_peer(lambda offset: legs_copy(row, n, offset).start())
+        own_legs(row, n).start()
 
     wait_all(table_ref, load_sem.at[2])
     wait_all(twiddle_ref, load_sem.at[3])
     both_rows(0)
-    lax.fori_loop(0, local_rows, leg_step, 0)
-    weight_start(5)
+
+    @pl.when(jnp.logical_not(far))
+    def _():
+        leg_step(0, 0)
+
+    both_rows(1)
+    both_rows(2)
+    weight_pass_on((4, 2))
+
+    @pl.when(far)
+    def _():
+        for n in range(len(LEG_GROUPS)):
+            def group_steps(row, carry):
+                leg_step(n, row)
+                return carry
+
+            lax.fori_loop(0, local_rows, group_steps, 0)
+
+    @pl.when(jnp.logical_not(far))
+    def _():
+        leg_step(1, 0)
+        leg_step(2, 0)
+        for n in range(len(LEG_GROUPS)):
+            leg_step(n, 1)
+
+    weight_start((5,))
 
     def map_step(n, carry):
         values = [
@@ -757,6 +840,7 @@
         return carry
 
     lax.fori_loop(0, local_rows, cur_start, 0)
+    weight_pass_on((5,))
 
     def est_copy(row, offset):
         return send_home(
@@ -833,6 +917,10 @@
     @pl.when(far)
     def _():
         wait_all(weights.at[:, 0], extra_left)
+
+    @pl.when(inner)
+    def _():
+        wait_all(relay_weights, pass_left)
 
     wait_all(weights.at[:, 0], weight_left)
     wait_all(spec_out.at[:, 0, 0:others], spec_left)
@@ -887,6 +975,7 @@
             pltpu.VMEM((6, local_rows, SIDE, SIDE), f32),
             slab, slab,
             pltpu.VMEM((3, 2, in_rows) + TILE, f32),
+            pltpu.VMEM((6, SIDE, SIDE), f32),
             pltpu.VMEM((3, local_rows, groups, 2) + TILE, f32),
             pltpu.VMEM((3, 2, groups) + TILE, f32),
             pltpu.VMEM((6, 3, SIDE, SIDE), f32),
@@ -896,8 +985,8 @@
             pltpu.VMEM((5, 2, total_rows) + TILE, f32),
             pltpu.VMEM((2, total_rows) + TILE, f32),
             chunk, lines, lines, chunk, final, final,
-            dma((3,)), dma((3,)), dma((3,)), dma((local_rows, len(WEIGHT_GROUPS))), dma((len(LEG_GROUPS),)),
-            dma((local_rows,)), dma((1,)), dma((1,)), dma((10,)), dma((4,)),
+            dma((3,)), dma((3,)), dma((3,)), dma((local_rows, len(WEIGHT_GROUPS))), dma((6,)), dma((len(LEG_GROUPS),)),
+            dma((local_rows,)), dma((1,)), dma((1,)), dma((11,)), dma((4,)),
         ],
         compiler_params=pltpu.CompilerParams(
             collective_id=0, has_side_effects=True, vmem_limit_bytes=60 * 1024 * 1024

time: 72.2 us -> 68.9 us (0.954)
  Pallas kernels: 70.3 us -> 67 us
    pallas_call x1, Pallas kernels: 70.3 us -> 67 us  [fused_body(): pl.pallas_call(lens_kernel, out_shape=jax.ShapeDtypeStruct((2,) + sky_map...]
where the time goes in v4:
time: 68.9 us; the launch traced here: 68.7 us
  Pallas kernels  67 us (97%)
  local copies, waits for them, and re-layouts  1.67 us (2%)
    pallas_call x1, Pallas kernels, fused_body(): pl.pallas_call(lens_kernel, out_shape=jax.ShapeDtypeStruct((2,) + sky_map...  67 us
    unnamed x1, local copies, waits for them, and re-layouts  1.67 us

profile of v4, /device:TPU:3, one launch (start us, length us, event | category | flops | bytes accessed | tf_op | source)
XLA Modules:
  0.0 68.7 jit_solution(13873536125340922664)
XLA Ops:
  0.0 67.0 %lens.1 = f32[2,8,4096]{2,1,0:T(8,128)} custom-call(s32[6]{0:T(128)} %cuts_ref.1, f32[3,8,4096]{2,1,0:T(8,128)} %sky_hbm.1, f32[3,2,16384]{2,1,0:T(2,128)} %filters_hbm.1, f32[2,2,16384]{2,1,0:T(2,128)} %wiener_hbm.1, f32[2,16384]{1,0:T(2,128)} %response_hbm.1, bf16[2,2,256,256]{3,2,1,0:T(8,128)(2,1)} %constant.4.clone.table_hbm, ...), custom_call_target="tpu_custom_call" | custom-call | tf_op jit(solution)/shard_map/lens/pallas_call | solution.py:966
  67.0 1.7 %copy.9 = f32[2,8,4096]{2,1,0:T(8,128)} copy(f32[2,8,4096]{2,1,0:T(8,128)} %lens.1) | data formatting | bytes 524288

commit v5 on v4

--- a/solution.py
+++ b/solution.py
@@ -363,15 +363,12 @@
     my_block = (2 * my_x + my_l) * rows_count + my_r
     stays = my_x == my_h
 
-    half_rows = total_rows // 2
-    corner = my_x + my_l == 0
-    far = jnp.logical_and(corner, my_y == 1)
-    near = jnp.logical_and(corner, my_y == 0)
+    outer = my_l == my_h
+    inner = my_l != my_h
     home_row = in_rows * my_r + 4 * my_h + 2 * my_l + my_x
-    first_row = jnp.where(corner, in_rows * my_c + 4 * (my_h + my_y - 2 * my_h * my_y), home_row)
 
     def signed(row):
-        return jnp.where(row < half_rows, row, row - total_rows)
+        return jnp.where(row < total_rows // 2, row, row - total_rows)
 
     def row_of(offset):
         return 2 * y_at[offset[1]] + c_at[offset[3]]
@@ -479,7 +476,7 @@
     freq_cols = jnp.where(column_ids < NC // 2, column_ids, column_ids - NC)
 
     def row_frequency(row):
-        return jnp.where(first_row == 0, -half_rows * row, signed(first_row) * (1 - 2 * row))
+        return signed(in_rows * my_r + 4 * my_l + 2 * (my_h + row - 2 * my_h * row) + my_x)
 
     wait_all(raw, load_sem.at[1])
 
@@ -498,60 +495,38 @@
         inside = (radius_home >= low * low) & (radius_home <= high * high)
         return inside.astype(jnp.float32)
 
-    home_slot = jnp.where(far, 2, 0)
-    outer = my_l == my_h
-    inner = my_l != my_h
+    home_slot = jnp.where(inner, 2, 0)
 
     def group_of(n):
         return [n in members for members in WEIGHT_GROUPS].index(True)
 
-    def weight_copy(n, source, low, sem):
-        cornered = my_x + low == 0
-        upper, lower = jnp.logical_and(cornered, my_y == 0), jnp.logical_and(cornered, my_y == 1)
-        other_r = jnp.where(upper, my_r + 2, jnp.where(lower, jnp.where(my_h == 0, my_r, 5 - my_r), 3 - my_r))
-        slot = jnp.where(upper, 0, 1)
+    def across(n, source, slot, left):
         return remote(
-            source, weights.at[n, slot], (sem, weight_sem.at[slot, group_of(n)]),
-            my_x, other_r, 2 * h_at[1] + jnp.where(my_x == 1, 1 - low, low),
+            source, weights.at[n, slot], (left, weight_sem.at[slot, group_of(n)]),
+            my_x, my_r, 2 * h_at[1] + my_h,
         )
 
     def own_weight(n):
-        return weight_copy(n, weights.at[n, home_slot], my_l, weight_left)
+        return across(n, weights.at[n, home_slot], 0, weight_left)
+
+    def near_copy(n):
+        return remote(
+            weights.at[n, home_slot], weights.at[n, 1], (extra_left, weight_sem.at[1, group_of(n)]),
+            my_x, my_r, 2 * my_h + l_at[1],
+        )
 
     def hand_copy(n):
         return remote(
             weights.at[n, home_slot], relay_weights.at[n], (weight_left, hand_sem.at[n]),
             my_x, my_r, 2 * my_h + l_at[1],
         )
-
-    def extra_copy(n):
-        return remote(
-            weights.at[n, home_slot], weights.at[n, 1], (extra_left, weight_sem.at[1, group_of(n)]),
-            my_x, jnp.where(my_h == 0, my_r - 2, 3 - my_r), my_z,
-        )
-
-    def weight_start(members):
-        @pl.when(outer)
-        def _():
-            for n in members:
-                hand_copy(n).start()
-
-        @pl.when(inner)
-        def _():
-            for n in members:
-                own_weight(n).start()
-
-        @pl.when(far)
-        def _():
-            for n in members:
-                extra_copy(n).start()
 
     def weight_pass_on(members):
         @pl.when(inner)
         def _():
             for n in members:
                 wait_all(relay_weights.at[n], hand_sem.at[n])
-                weight_copy(n, relay_weights.at[n], l_at[1], pass_left).start()
+                across(n, relay_weights.at[n], 1, pass_left).start()
 
     pol = mask(1)
     weights[0, home_slot] = mask(0) * weight_ref[0, my_x].T
@@ -565,6 +540,7 @@
         slab_start(1)
         slab_start(2)
         for n in WEIGHT_ORDER[:5]:
+            near_copy(n).start()
             own_weight(n).start()
 
     @pl.when(jnp.logical_and(outer, jnp.logical_not(stays)))
@@ -578,37 +554,32 @@
     @pl.when(jnp.logical_and(inner, stays))
     def _():
         own_weight(0).start()
+        for n in WEIGHT_ORDER[:5]:
+            near_copy(n).start()
 
     @pl.when(jnp.logical_and(outer, stays))
     def _():
         hand_copy(0).start()
         hand_copy(3).start()
 
-    def owner(k):
-        return k // 8 * fields_count + 2 * (k % 2) + k // 2 % 2
-
     def place(k, half):
-        if k % 4 == 0:
-            base = k % half_rows if k <= half_rows else total_rows - k
-            upper = half if base % 8 == 0 else 1 - half
-            return int(k >= half_rows), (base // in_rows + 2 * upper) * fields_count
-        away = 1 - half if k // 4 % 2 else half
-        return away, owner(k) + away * (owner(total_rows - k) - owner(k))
-
-    def spec_copy(field, offset):
+        return 1 - half if k // 2 % 2 else half, k // in_rows * fields_count + 2 * (k % 2) + k // 4 % 2
+
+    def spec_copy(field, row, offset):
         return send(
-            offset, spec_out.at[field, 0, peer_of(offset)], spec_in.at[field, :, my_block],
+            offset, spec_out.at[field, row, peer_of(offset)], spec_in.at[field, row, :, my_block],
             (spec_left, spec_sem.at[field]),
         )
 
-    def own_spec(field):
+    def own_spec(field, row):
         return pltpu.make_async_copy(
-            spec_out.at[field, 0, me], spec_in.at[field, :, my_block], spec_sem.at[field]
+            spec_out.at[field, row, me], spec_in.at[field, row, :, my_block], spec_sem.at[field]
         )
 
     def spec_start(field):
-        each_peer(lambda offset: spec_copy(field, offset).start())
-        own_spec(field).start()
+        for row in range(local_rows):
+            each_peer(lambda offset: spec_copy(field, row, offset).start())
+            own_spec(field, row).start()
 
     def row_step(field):
         @pl.when(stays)
@@ -632,14 +603,10 @@
         values = [
             (slab_in[y // in_rows, field, y % in_rows], None) for y in range(total_rows)
         ]
-        lines = short_transform(values, -1)
-        lines[0] = (lines[0][0], lines[half_rows][0])
-        for k, (real, imag) in enumerate(lines):
-            if k % 4 == 0 and k >= half_rows:
-                continue
+        for k, (real, imag) in enumerate(short_transform(values, -1)):
             local, device = place(k, my_h)
             spec_out[field, local, device, 0] = real
-            spec_out[field, local, device, 1] = imag
+            spec_out[field, local, device, 1] = jnp.zeros_like(real) if imag is None else imag
         spec_start(field)
 
     for field in range(3):
@@ -649,11 +616,6 @@
     def _():
         hand_copy(4).start()
         hand_copy(2).start()
-
-    @pl.when(far)
-    def _():
-        for n in WEIGHT_ORDER[:5]:
-            extra_copy(n).start()
 
     weight_pass_on((0, 3, 1))
 
@@ -708,7 +670,7 @@
     def wait_weights(group, row):
         members = WEIGHT_GROUPS[group]
 
-        @pl.when(jnp.logical_or(row == 1, far))
+        @pl.when(jnp.logical_or(row == 1, inner))
         def _():
             wait_all(weights.at[0:len(members), row], weight_sem.at[row, group])
 
@@ -717,16 +679,11 @@
         along_y = (2 * row_frequency(row)).astype(jnp.float32) / total_rows
         return along_x, along_y
 
-    packed = jnp.where(first_row == 0, 0.5, 0.0)
-
     def both_rows(field):
         wait_all(spec_in.at[field], spec_sem.at[field])
-        line = spec_in[field].reshape(2 * SIDE, SIDE)
-        (ar, ai), (br, bi) = long_forward([line, jnp.concatenate([line[:SIDE], -line[SIDE:]], axis=0)])
-        modes[field, 0, 0] = (1.0 - packed) * ar + packed * br
-        modes[field, 0, 1] = (1.0 - packed) * ai + packed * bi
-        modes[field, 1, 0] = (1.0 - 2.0 * packed) * br + packed * (ai - bi)
-        modes[field, 1, 1] = (1.0 - 2.0 * packed) * bi + packed * (br - ar)
+        pairs = long_forward([spec_in[field, row].reshape(2 * SIDE, SIDE) for row in range(local_rows)])
+        for row, pair in enumerate(pairs):
+            modes[field, row, 0], modes[field, row, 1] = pair
 
     def leg_step(n, row):
         scaled = row_ratio * row_frequency(row)
@@ -769,31 +726,38 @@
     wait_all(twiddle_ref, load_sem.at[3])
     both_rows(0)
 
-    @pl.when(jnp.logical_not(far))
+    @pl.when(outer)
     def _():
         leg_step(0, 0)
+        leg_step(0, 1)
 
     both_rows(1)
     both_rows(2)
     weight_pass_on((4, 2))
 
-    @pl.when(far)
-    def _():
-        for n in range(len(LEG_GROUPS)):
-            def group_steps(row, carry):
-                leg_step(n, row)
-                return carry
-
-            lax.fori_loop(0, local_rows, group_steps, 0)
-
-    @pl.when(jnp.logical_not(far))
-    def _():
-        leg_step(1, 0)
-        leg_step(2, 0)
-        for n in range(len(LEG_GROUPS)):
-            leg_step(n, 1)
-
-    weight_start((5,))
+    @pl.when(inner)
+    def _():
+        leg_step(0, 0)
+
+    def later_steps(row, carry):
+        @pl.when(jnp.logical_and(inner, row == 1))
+        def _():
+            leg_step(0, 1)
+
+        leg_step(1, row)
+        leg_step(2, row)
+        return carry
+
+    lax.fori_loop(0, local_rows, later_steps, 0)
+
+    @pl.when(inner)
+    def _():
+        near_copy(5).start()
+        own_weight(5).start()
+
+    @pl.when(outer)
+    def _():
+        hand_copy(5).start()
 
     def map_step(n, carry):
         values = [
@@ -842,17 +806,18 @@
     lax.fori_loop(0, local_rows, cur_start, 0)
     weight_pass_on((5,))
 
+    HOME_OFFSETS = sorted(PEERS, key=lambda offset: -offset[0])
+    ORIGIN = (0, 0, 0, 0)
+
     def est_copy(row, offset):
-        return send_home(
-            offset, est_out.at[row, :, peer_block(offset)], est_in.at[row, me],
-            (est_left, est_sem.at[0]),
-        )
-
-    ORIGIN = (0, 0, 0, 0)
+        r, z = row_of(offset), 2 * h_at[offset[0]] + l_at[offset[2]]
+        return remote(
+            est_out.at[row, :, z * rows_count + r], est_in.at[row, me], (est_left, est_sem.at[0]), my_h, r, z
+        )
 
     def own_est(row):
         return pltpu.make_async_copy(
-            est_out.at[row, :, my_block], est_in.at[row, me], est_sem.at[0]
+            est_out.at[row, :, my_z * rows_count + my_r], est_in.at[row, me], est_sem.at[0]
         )
 
     def estimate_step(row, carry):
@@ -864,7 +829,8 @@
         w = weights[5, row]
         estimate = complex_mul((w * modes[0], w * modes[1]), (along_y, along_x))
         (est_out[row],) = long_inverse([estimate])
-        each_peer(lambda offset: est_copy(row, offset).start())
+        for offset in HOME_OFFSETS:
+            est_copy(row, offset).start()
 
         @pl.when(stays)
         def _():
@@ -914,16 +880,13 @@
         wait_all(relay_buf, relay_left)
         wait_all(est_out, est_left)
 
-    @pl.when(far)
-    def _():
-        wait_all(weights.at[:, 0], extra_left)
-
     @pl.when(inner)
     def _():
         wait_all(relay_weights, pass_left)
+        wait_all(relay_weights, extra_left)
 
     wait_all(weights.at[:, 0], weight_left)
-    wait_all(spec_out.at[:, 0, 0:others], spec_left)
+    wait_all(spec_out.at[:, :, 0:others], spec_left)
     wait_all(legs_out.at[:, :, :, 0:others], legs_left)
     wait_all(cur_out.at[:, 0:others], cur_left)
     wait_all(fin_in, fin_sem.at[0])
@@ -977,7 +940,7 @@
             pltpu.VMEM((3, 2, in_rows) + TILE, f32),
             pltpu.VMEM((6, SIDE, SIDE), f32),
             pltpu.VMEM((3, local_rows, groups, 2) + TILE, f32),
-            pltpu.VMEM((3, 2, groups) + TILE, f32),
+            pltpu.VMEM((3, local_rows, 2, groups) + TILE, f32),
             pltpu.VMEM((6, 3, SIDE, SIDE), f32),
             pltpu.VMEM((3, local_rows, 2, SIDE, SIDE), f32),
             pltpu.VMEM((local_rows, 5, 2, groups) + TILE, f32),

time: 68.9 us -> 67.6 us (0.981)
  Pallas kernels: 67 us -> 65.8 us
    pallas_call x1, Pallas kernels: 67 us -> 65.8 us  [fused_body(): pl.pallas_call(lens_kernel, out_shape=jax.ShapeDtypeStruct((2,) + sky_map...]
where the time goes in v5:
time: 67.6 us; the launch traced here: 67.4 us
  Pallas kernels  65.8 us (97%)
  local copies, waits for them, and re-layouts  1.67 us (2%)
    pallas_call x1, Pallas kernels, fused_body(): pl.pallas_call(lens_kernel, out_shape=jax.ShapeDtypeStruct((2,) + sky_map...  65.8 us
    unnamed x1, local copies, waits for them, and re-layouts  1.67 us

profile of v5, /device:TPU:3, one launch (start us, length us, event | category | flops | bytes accessed | tf_op | source)
XLA Modules:
  0.0 67.4 jit_solution(18345862462466695623)
XLA Ops:
  0.0 65.8 %lens.1 = f32[2,8,4096]{2,1,0:T(8,128)} custom-call(s32[6]{0:T(128)} %cuts_ref.1, f32[3,8,4096]{2,1,0:T(8,128)} %sky_hbm.1, f32[3,2,16384]{2,1,0:T(2,128)} %filters_hbm.1, f32[2,2,16384]{2,1,0:T(2,128)} %wiener_hbm.1, f32[2,16384]{1,0:T(2,128)} %response_hbm.1, bf16[2,2,256,256]{3,2,1,0:T(8,128)(2,1)} %constant.4.clone.table_hbm, ...), custom_call_target="tpu_custom_call" | custom-call | tf_op jit(solution)/shard_map/lens/pallas_call | solution.py:929
  65.8 1.7 %copy.9 = f32[2,8,4096]{2,1,0:T(8,128)} copy(f32[2,8,4096]{2,1,0:T(8,128)} %lens.1) | data formatting | bytes 524288

commit v6 on v5

--- a/solution.py
+++ b/solution.py
@@ -752,12 +752,12 @@
 
     @pl.when(inner)
     def _():
+        own_weight(5).start()
         near_copy(5).start()
-        own_weight(5).start()
 
     @pl.when(outer)
     def _():
-        hand_copy(5).start()
+        across(5, weights.at[5, 0], 1, weight_left).start()
 
     def map_step(n, carry):
         values = [
@@ -804,67 +804,77 @@
         return carry
 
     lax.fori_loop(0, local_rows, cur_start, 0)
-    weight_pass_on((5,))
 
     HOME_OFFSETS = sorted(PEERS, key=lambda offset: -offset[0])
     ORIGIN = (0, 0, 0, 0)
 
-    def est_copy(row, offset):
+    def part_of(sub):
+        return slice(sub * TILE[0] // 2, (sub + 1) * TILE[0] // 2)
+
+    def est_copy(row, offset, sub):
         r, z = row_of(offset), 2 * h_at[offset[0]] + l_at[offset[2]]
         return remote(
-            est_out.at[row, :, z * rows_count + r], est_in.at[row, me], (est_left, est_sem.at[0]), my_h, r, z
-        )
-
-    def own_est(row):
+            est_out.at[row, :, z * rows_count + r, part_of(sub)], est_in.at[row, me, :, part_of(sub)],
+            (est_left, est_sem.at[sub]), my_h, r, z,
+        )
+
+    def own_est(row, sub):
         return pltpu.make_async_copy(
-            est_out.at[row, :, my_z * rows_count + my_r], est_in.at[row, me], est_sem.at[0]
-        )
-
-    def estimate_step(row, carry):
+            est_out.at[row, :, my_z * rows_count + my_r, part_of(sub)], est_in.at[row, me, :, part_of(sub)],
+            est_sem.at[sub],
+        )
+
+    def est_start(row, sub):
+        for offset in HOME_OFFSETS:
+            est_copy(row, offset, sub).start()
+
+        @pl.when(stays)
+        def _():
+            own_est(row, sub).start()
+
+        @pl.when(jnp.logical_not(stays))
+        def _():
+            est_copy(row, ORIGIN, sub).start()
+
+    def estimate_step(row):
         wait_all(cur_in.at[row], cur_sem.at[row])
         wait_weights(3, row)
-
         (modes,) = long_forward([cur_in[row].reshape(2 * SIDE, SIDE)])
         along_x, along_y = slopes(row)
         w = weights[5, row]
         estimate = complex_mul((w * modes[0], w * modes[1]), (along_y, along_x))
         (est_out[row],) = long_inverse([estimate])
-        for offset in HOME_OFFSETS:
-            est_copy(row, offset).start()
-
-        @pl.when(stays)
-        def _():
-            own_est(row).start()
-
-        @pl.when(jnp.logical_not(stays))
-        def _():
-            est_copy(row, ORIGIN).start()
-
-        return carry
-
-    lax.fori_loop(0, local_rows, estimate_step, 0)
-
-    wait_all(est_in, est_sem.at[0])
-    values = [
-        (est_in[place(k, my_x) + (0,)], est_in[place(k, my_x) + (1,)])
-        for k in range(total_rows)
-    ]
-    for y, (real, imag) in enumerate(short_transform(values, 1)):
-        fin_out[y // in_rows, 0, y % in_rows] = real
-        fin_out[y // in_rows, 1, y % in_rows] = imag
-
-    def fin_copy(offset):
+        est_start(row, 0)
+
+    for row in range(local_rows):
+        estimate_step(row)
+    for row in range(local_rows):
+        est_start(row, 1)
+
+    def fin_copy(offset, sub):
         r = row_of(offset)
         return remote(
-            fin_out.at[r], fin_in.at[my_r], (fin_left, fin_sem.at[0]), my_x, r, my_z
-        )
-
-    for offset in ROW_OFFSETS[1:]:
-        fin_copy(offset).start()
-    own_fin = pltpu.make_async_copy(
-        fin_out.at[my_r], fin_in.at[my_r], fin_sem.at[0]
-    )
-    own_fin.start()
+            fin_out.at[r, :, :, part_of(sub)], fin_in.at[my_r, :, :, part_of(sub)],
+            (fin_left, fin_sem.at[sub]), my_x, r, my_z,
+        )
+
+    def own_fin(sub):
+        return pltpu.make_async_copy(
+            fin_out.at[my_r, :, :, part_of(sub)], fin_in.at[my_r, :, :, part_of(sub)], fin_sem.at[sub]
+        )
+
+    for sub in range(2):
+        wait_all(est_in.at[:, :, :, part_of(sub)], est_sem.at[sub])
+        values = []
+        for k in range(total_rows):
+            local, device = place(k, my_x)
+            values.append(tuple(est_in[local, device, part, part_of(sub)] for part in range(2)))
+        for y, pair in enumerate(short_transform(values, 1)):
+            for part in range(2):
+                fin_out[y // in_rows, part, y % in_rows, part_of(sub)] = pair[part]
+        for offset in ROW_OFFSETS[1:]:
+            fin_copy(offset, sub).start()
+        own_fin(sub).start()
 
     others = groups - 1
 
@@ -882,17 +892,19 @@
 
     @pl.when(inner)
     def _():
-        wait_all(relay_weights, pass_left)
+        wait_all(relay_weights.at[0:5], pass_left)
         wait_all(relay_weights, extra_left)
 
     wait_all(weights.at[:, 0], weight_left)
     wait_all(spec_out.at[:, :, 0:others], spec_left)
     wait_all(legs_out.at[:, :, :, 0:others], legs_left)
     wait_all(cur_out.at[:, 0:others], cur_left)
-    wait_all(fin_in, fin_sem.at[0])
-    for part in range(2):
-        for t in range(tiles):
-            out_ref[part, :, t * SIDE:(t + 1) * SIDE] = fin_in[t // 8, part, :, t % 8, :]
+    for sub in range(2):
+        wait_all(fin_in.at[:, :, :, part_of(sub)], fin_sem.at[sub])
+        for part in range(2):
+            for t in range(tiles):
+                if t % TILE[0] * 2 // TILE[0] == sub:
+                    out_ref[part, :, t * SIDE:(t + 1) * SIDE] = fin_in[t // TILE[0], part, :, t % TILE[0], :]
 
     wait_all(fin_out.at[0:3], fin_left)
 
@@ -949,7 +961,7 @@
             pltpu.VMEM((2, total_rows) + TILE, f32),
             chunk, lines, lines, chunk, final, final,
             dma((3,)), dma((3,)), dma((3,)), dma((local_rows, len(WEIGHT_GROUPS))), dma((6,)), dma((len(LEG_GROUPS),)),
-            dma((local_rows,)), dma((1,)), dma((1,)), dma((11,)), dma((4,)),
+            dma((local_rows,)), dma((2,)), dma((2,)), dma((11,)), dma((4,)),
         ],
         compiler_params=pltpu.CompilerParams(
             collective_id=0, has_side_effects=True, vmem_limit_bytes=60 * 1024 * 1024

time: 67.6 us -> 66.4 us (0.982)
  Pallas kernels: 65.8 us -> 64.6 us
    pallas_call x1, Pallas kernels: 65.8 us -> 64.6 us  [fused_body(): pl.pallas_call(lens_kernel, out_shape=jax.ShapeDtypeStruct((2,) + sky_map...]
where the time goes in v6:
time: 66.4 us; the launch traced here: 66.3 us
  Pallas kernels  64.6 us (97%)
  local copies, waits for them, and re-layouts  1.67 us (3%)
    pallas_call x1, Pallas kernels, fused_body(): pl.pallas_call(lens_kernel, out_shape=jax.ShapeDtypeStruct((2,) + sky_map...  64.6 us
    unnamed x1, local copies, waits for them, and re-layouts  1.67 us

profile of v6, /device:TPU:3, one launch (start us, length us, event | category | flops | bytes accessed | tf_op | source)
XLA Modules:
  0.0 66.3 jit_solution(4665703346423652327)
XLA Ops:
  0.0 64.6 %lens.1 = f32[2,8,4096]{2,1,0:T(8,128)} custom-call(s32[6]{0:T(128)} %cuts_ref.1, f32[3,8,4096]{2,1,0:T(8,128)} %sky_hbm.1, f32[3,2,16384]{2,1,0:T(2,128)} %filters_hbm.1, f32[2,2,16384]{2,1,0:T(2,128)} %wiener_hbm.1, f32[2,16384]{1,0:T(2,128)} %response_hbm.1, bf16[2,2,256,256]{3,2,1,0:T(8,128)(2,1)} %constant.4.clone.table_hbm, ...), custom_call_target="tpu_custom_call" | custom-call | tf_op jit(solution)/shard_map/lens/pallas_call | solution.py:941
  64.6 1.7 %copy.9 = f32[2,8,4096]{2,1,0:T(8,128)} copy(f32[2,8,4096]{2,1,0:T(8,128)} %lens.1) | data formatting | bytes 524288

commit v7 on v6

--- a/solution.py
+++ b/solution.py
@@ -337,18 +337,19 @@
 
 
 BITS = (0, 1)
+SUBS = 2
 OFFSETS = [
     (c, a1, e, a0) for a0 in BITS for c, a1, e in
     ((1, 1, 1), (1, 0, 0), (0, 1, 0), (0, 0, 1), (1, 1, 0), (0, 1, 1), (1, 0, 1), (0, 0, 0))
 ]
-PEERS = [offset for offset in OFFSETS if any(offset)]
+PEERS = sorted((offset for offset in OFFSETS if any(offset)), key=lambda offset: -sum(offset[:3]))
 WEIGHT_ORDER = (0, 3, 1, 4, 2, 5)
 
 
 def lens_kernel(
     cuts_ref, sky_hbm, filters_hbm, wiener_hbm, response_hbm, table_hbm, twiddle_hbm, out_ref,
     table_ref, twiddle_ref, sky_ref, raw, weight_ref, slab_out, slab_in, relay_buf, relay_weights, spec_out, spec_in, weights, modes, legs_out, legs_in,
-    maps, current, cur_out, cur_in, est_out, est_in, fin_out, fin_in,
+    maps, cur_out, cur_in, est_out, est_in, fin_out, fin_in,
     slab_sem, relay_sem, spec_sem, weight_sem, hand_sem, legs_sem, cur_sem, est_sem, fin_sem, send_sem, load_sem,
 ):
     rows_count, fields_count, local_rows = 4, 4, 2
@@ -753,7 +754,6 @@
     @pl.when(inner)
     def _():
         own_weight(5).start()
-        near_copy(5).start()
 
     @pl.when(outer)
     def _():
@@ -773,16 +773,12 @@
         wait_all(legs_in.at[:, :, first:first + count], legs_sem.at[g])
         lax.fori_loop(first, first + count, map_step, 0)
 
-    def product_step(y, carry):
+    def product(y):
         a, g, h3, h1, p = [(maps[n, 0, y], maps[n, 1, y]) for n in range(5)]
         ag, ph, hp = complex_mul(a, g), conj_mul(p, h3), conj_mul(h1, p)
-        current[0, y] = ag[0] + 0.5 * (ph[0] + hp[0])
-        current[1, y] = ag[1] + 0.5 * (ph[1] + hp[1])
-        return carry
-
-    lax.fori_loop(0, total_rows, product_step, 0)
-
-    values = [(current[0, y], current[1, y]) for y in range(total_rows)]
+        return ag[0] + 0.5 * (ph[0] + hp[0]), ag[1] + 0.5 * (ph[1] + hp[1])
+
+    values = [product(y) for y in range(total_rows)]
     for k, (real, imag) in enumerate(short_transform(values, -1)):
         cur_out[place(k, my_h) + (0,)] = real
         cur_out[place(k, my_h) + (1,)] = imag
@@ -805,11 +801,16 @@
 
     lax.fori_loop(0, local_rows, cur_start, 0)
 
+    @pl.when(inner)
+    def _():
+        near_copy(5).start()
+
+
     HOME_OFFSETS = sorted(PEERS, key=lambda offset: -offset[0])
     ORIGIN = (0, 0, 0, 0)
 
     def part_of(sub):
-        return slice(sub * TILE[0] // 2, (sub + 1) * TILE[0] // 2)
+        return slice(sub * TILE[0] // SUBS, (sub + 1) * TILE[0] // SUBS)
 
     def est_copy(row, offset, sub):
         r, z = row_of(offset), 2 * h_at[offset[0]] + l_at[offset[2]]
@@ -848,8 +849,9 @@
 
     for row in range(local_rows):
         estimate_step(row)
-    for row in range(local_rows):
-        est_start(row, 1)
+    for sub in range(1, SUBS):
+        for row in range(local_rows):
+            est_start(row, sub)
 
     def fin_copy(offset, sub):
         r = row_of(offset)
@@ -863,7 +865,7 @@
             fin_out.at[my_r, :, :, part_of(sub)], fin_in.at[my_r, :, :, part_of(sub)], fin_sem.at[sub]
         )
 
-    for sub in range(2):
+    for sub in range(SUBS):
         wait_all(est_in.at[:, :, :, part_of(sub)], est_sem.at[sub])
         values = []
         for k in range(total_rows):
@@ -899,11 +901,11 @@
     wait_all(spec_out.at[:, :, 0:others], spec_left)
     wait_all(legs_out.at[:, :, :, 0:others], legs_left)
     wait_all(cur_out.at[:, 0:others], cur_left)
-    for sub in range(2):
+    for sub in range(SUBS):
         wait_all(fin_in.at[:, :, :, part_of(sub)], fin_sem.at[sub])
         for part in range(2):
             for t in range(tiles):
-                if t % TILE[0] * 2 // TILE[0] == sub:
+                if t % TILE[0] * SUBS // TILE[0] == sub:
                     out_ref[part, :, t * SIDE:(t + 1) * SIDE] = fin_in[t // TILE[0], part, :, t % TILE[0], :]
 
     wait_all(fin_out.at[0:3], fin_left)
@@ -958,10 +960,9 @@
             pltpu.VMEM((local_rows, 5, 2, groups) + TILE, f32),
             pltpu.VMEM((local_rows, groups, 5, 2) + TILE, f32),
             pltpu.VMEM((5, 2, total_rows) + TILE, f32),
-            pltpu.VMEM((2, total_rows) + TILE, f32),
             chunk, lines, lines, chunk, final, final,
             dma((3,)), dma((3,)), dma((3,)), dma((local_rows, len(WEIGHT_GROUPS))), dma((6,)), dma((len(LEG_GROUPS),)),
-            dma((local_rows,)), dma((2,)), dma((2,)), dma((11,)), dma((4,)),
+            dma((local_rows,)), dma((SUBS,)), dma((SUBS,)), dma((11,)), dma((4,)),
         ],
         compiler_params=pltpu.CompilerParams(
             collective_id=0, has_side_effects=True, vmem_limit_bytes=60 * 1024 * 1024

time: 66.4 us -> 65.8 us (level)
  no operation moved by 1% of the time
where the time goes in v7:
time: 65.8 us; the launch traced here: 65.7 us
  Pallas kernels  64 us (97%)
  local copies, waits for them, and re-layouts  1.67 us (3%)
    pallas_call x1, Pallas kernels, fused_body(): pl.pallas_call(lens_kernel, out_shape=jax.ShapeDtypeStruct((2,) + sky_map...  64 us
    unnamed x1, local copies, waits for them, and re-layouts  1.67 us

profile of v7, /device:TPU:3, one launch (start us, length us, event | category | flops | bytes accessed | tf_op | source)
XLA Modules:
  0.0 65.7 jit_solution(16173050691908180724)
XLA Ops:
  0.0 64.0 %lens.1 = f32[2,8,4096]{2,1,0:T(8,128)} custom-call(s32[6]{0:T(128)} %cuts_ref.1, f32[3,8,4096]{2,1,0:T(8,128)} %sky_hbm.1, f32[3,2,16384]{2,1,0:T(2,128)} %filters_hbm.1, f32[2,2,16384]{2,1,0:T(2,128)} %wiener_hbm.1, f32[2,16384]{1,0:T(2,128)} %response_hbm.1, bf16[2,2,256,256]{3,2,1,0:T(8,128)(2,1)} %constant.4.clone.table_hbm, ...), custom_call_target="tpu_custom_call" | custom-call | tf_op jit(solution)/shard_map/lens/pallas_call | solution.py:943
  64.0 1.7 %copy.9 = f32[2,8,4096]{2,1,0:T(8,128)} copy(f32[2,8,4096]{2,1,0:T(8,128)} %lens.1) | data formatting | bytes 524288

commit v8 on v7

--- a/solution.py
+++ b/solution.py
@@ -799,7 +799,8 @@
         own_cur(row).start()
         return carry
 
-    lax.fori_loop(0, local_rows, cur_start, 0)
+    for row in range(local_rows):
+        cur_start(row, 0)
 
     @pl.when(inner)
     def _():

time: 65.8 us -> 65.8 us (level)
  no operation moved by 1% of the time
where the time goes in v8:
time: 65.8 us; the launch traced here: 65.7 us
  Pallas kernels  64 us (97%)
  local copies, waits for them, and re-layouts  1.67 us (3%)
    pallas_call x1, Pallas kernels, fused_body(): pl.pallas_call(lens_kernel, out_shape=jax.ShapeDtypeStruct((2,) + sky_map...  64 us
    unnamed x1, local copies, waits for them, and re-layouts  1.67 us

profile of v8, /device:TPU:3, one launch (start us, length us, event | category | flops | bytes accessed | tf_op | source)
XLA Modules:
  0.0 65.7 jit_solution(15440469844925309481)
XLA Ops:
  0.0 64.0 %lens.1 = f32[2,8,4096]{2,1,0:T(8,128)} custom-call(s32[6]{0:T(128)} %cuts_ref.1, f32[3,8,4096]{2,1,0:T(8,128)} %sky_hbm.1, f32[3,2,16384]{2,1,0:T(2,128)} %filters_hbm.1, f32[2,2,16384]{2,1,0:T(2,128)} %wiener_hbm.1, f32[2,16384]{1,0:T(2,128)} %response_hbm.1, bf16[2,2,256,256]{3,2,1,0:T(8,128)(2,1)} %constant.4.clone.table_hbm, ...), custom_call_target="tpu_custom_call" | custom-call | tf_op jit(solution)/shard_map/lens/pallas_call | solution.py:944
  64.0 1.7 %copy.9 = f32[2,8,4096]{2,1,0:T(8,128)} copy(f32[2,8,4096]{2,1,0:T(8,128)} %lens.1) | data formatting | bytes 524288
